TPU v7x, 32 devices: a whole 2x2x4 slice. The times are simulated.
32 devices in a mesh: shard: 4 (over x, core), context: 2 (over y), tensor: 4 (over z).
Axes of the slice: x: 2, y: 2, z: 4, core: 2. Of those that a mesh axis runs over, the one named last changes fastest.
Arguments:
- hidden: bfloat16 [4, 1024, 2048], P('shard', 'context'), may hold values from -6 to 6
- norm1_gain: float32 [2048], replicated, may hold values from 0.5 to 1.5
- w_query: bfloat16 [2048, 2048], P('shard', 'tensor'), may hold values from -0.125 to 0.125
- w_key: bfloat16 [2048, 2048], P('shard', 'tensor'), may hold values from -0.125 to 0.125
- w_value: bfloat16 [2048, 2048], P('shard', 'tensor'), may hold values from -0.125 to 0.125
- query_gain: float32 [2048], P('tensor'), may hold values from 0.5 to 1.5
- key_gain: float32 [2048], P('tensor'), may hold values from 0.5 to 1.5
- w_output: bfloat16 [2048, 2048], P('tensor', 'shard'), may hold values from -0.5 to 0.5
- norm2_gain: float32 [2048], replicated, may hold values from 0.5 to 1.5
- w_router: bfloat16 [2048, 16], P('shard'), may hold values from -0.125 to 0.125
- w_gate: bfloat16 [16, 2048, 1024], P(None, 'shard', 'tensor'), may hold values from -0.125 to 0.125
- w_up: bfloat16 [16, 2048, 1024], P(None, 'shard', 'tensor'), may hold values from -0.125 to 0.125
- w_down: bfloat16 [16, 1024, 2048], P(None, 'tensor', 'shard'), may hold values from -1.5 to 1.5
- seq_lengths: int32 [4], P('shard'), may hold values from 256 to 1024, as said below
- expert_routes: int32 [4, 1024, 8], P('shard', 'context'), may hold values from 0 to 15, all different within a row
- out_grad: bfloat16 [4, 1024, 2048], P('shard', 'context'), may hold values from -6 to 6
Outputs:
- block_out: bfloat16 [4, 1024, 2048], P('shard', 'context')
- input_grad: bfloat16 [4, 1024, 2048], P('shard', 'context')
- norm1_gain_grad: float32 [2048], replicated
- w_query_grad: float32 [2048, 2048], P('shard', 'tensor')
- w_key_grad: float32 [2048, 2048], P('shard', 'tensor')
- w_value_grad: float32 [2048, 2048], P('shard', 'tensor')
- query_gain_grad: float32 [2048], P('tensor')
- key_gain_grad: float32 [2048], P('tensor')
- w_output_grad: float32 [2048, 2048], P('tensor', 'shard')
- norm2_gain_grad: float32 [2048], replicated
- w_router_grad: float32 [2048, 16], P('shard')
- w_gate_grad: float32 [16, 2048, 1024], P(None, 'shard', 'tensor')
- w_up_grad: float32 [16, 2048, 1024], P(None, 'shard', 'tensor')
- w_down_grad: float32 [16, 1024, 2048], P(None, 'tensor', 'shard')
Inputs may be any that keep to these rules, and one draw needn't show every extreme that they name: `seq_lengths`: each slot's valid positions come first; some slot has all 1024 in every draw. `expert_routes`: each position names 8 different experts.
All inputs are finite; a program needn't handle non-finite values.
Results may differ from a plain program's by a relative error of at most 0.018.
Values may be sent and summed in bfloat16 or wider, within the bound.
A program may use at most 320 MiB of HBM per device.

v0:
```python
import functools

import jax
import jax.numpy as jnp
from jax import lax
from jax.experimental import pallas as pl
from jax.experimental.pallas import tpu as pltpu
from jax.sharding import PartitionSpec as P


HEAD_DIM = 128
EPSILON = 1e-05
GROUP = 4
f32 = jnp.float32
bf16 = jnp.bfloat16


def nn(a, b):
    return lax.dot_general(a, b, (((1,), (0,)), ((), ())), preferred_element_type=f32)


def nt(a, b):
    return lax.dot_general(a, b, (((1,), (1,)), ((), ())), preferred_element_type=f32)


def tn(a, b):
    return lax.dot_general(a, b, (((0,), (0,)), ((), ())), preferred_element_type=f32)


def moe_kernel(
    first, partial, final, base, count,
    h_ref, g_ref, coef_ref, w_own, w_core, w_x, w_xc, *refs,
):
    refs = list(refs)
    sums_in = [] if first else [refs.pop(0) for _ in range(3)]
    grads_in = refs.pop(0) if partial else None
    moe_ref, dh_ref, dc_ref = (refs.pop(0) for _ in range(3))
    outs = [refs.pop(0) for _ in range(2 if final else 1)]
    wbuf, wsems, *swap = refs
    step = pl.program_id(0)
    chunk = h_ref.shape[1] // 4
    slot = lax.rem(step, 2)
    before = 1 - slot

    def fetch(at, slot, act):
        for piece, src in enumerate((w_own.at[:, base + at], w_core.at[:, base + at], w_x.at[:, at], w_xc.at[:, at])):
            dst = wbuf.at[slot, :, pl.ds(piece * chunk, chunk)]
            act(pltpu.make_async_copy(src, dst, wsems.at[slot, piece]))

    if final:
        keep, send, got, send_sems, got_sems, free = swap
        me = lax.axis_index("shard")
        partner = {"shard": me + 1 - 2 * lax.rem(me, 2)}

        def swap_copy(slot):
            return pltpu.make_async_remote_copy(
                src_ref=send.at[slot],
                dst_ref=got.at[slot],
                send_sem=send_sems.at[slot],
                recv_sem=got_sems.at[slot],
                device_id=partner,
                device_id_type=pl.DeviceIdType.MESH,
            )

    @pl.when(step == 0)
    def _():
        fetch(0, 0, lambda c: c.start())
        if final:
            barrier = pltpu.get_barrier_semaphore()
            pl.semaphore_signal(
                barrier, inc=1, device_id=partner, device_id_type=pl.DeviceIdType.MESH
            )
            pl.semaphore_wait(barrier, 1)
        for i, ref in enumerate((moe_ref, dh_ref, dc_ref)):
            ref[...] = jnp.zeros_like(ref) if first else sums_in[i][...]

    @pl.when(step + 1 < count)
    def _():
        fetch(step + 1, before, lambda c: c.start())

    @pl.when(step < count)
    def _():
        fetch(step, slot, lambda c: c.wait())
        lanes = lax.broadcasted_iota(jnp.int32, coef_ref.shape, 1)
        picked = lanes == base + step
        coef = jnp.sum(jnp.where(picked, coef_ref[...], 0.0), axis=1, keepdims=True)
        wg, wu, wd = wbuf.at[slot, 0], wbuf.at[slot, 1], wbuf.at[slot, 2]
        gate = nn(h_ref[...], wg[...])
        up = nn(h_ref[...], wu[...])
        dz_plain = nn(g_ref[...], wd[...])
        sig = jax.nn.sigmoid(gate)
        act = gate * sig
        z = act * up
        z_coef = (z * coef).astype(bf16)
        dcoef = jnp.sum(z * dz_plain, axis=1, keepdims=True)
        dc_ref[...] += jnp.where(picked, dcoef, 0.0)
        dz = dz_plain * coef
        dgate = (dz * up * (sig * (1.0 + gate * (1.0 - sig)))).astype(bf16)
        dup = (dz * act).astype(bf16)
        for j in range(4):
            rows = slice(j * chunk, (j + 1) * chunk)
            moe_ref[:, rows] += nt(z_coef, wd[rows, :])
            dh_ref[:, rows] += nt(dgate, wg[rows, :]) + nt(dup, wu[rows, :])
            for i, (left, right) in enumerate(((dgate, h_ref), (dup, h_ref), (z_coef, g_ref))):
                grad = tn(left, right[:, rows])
                if partial:
                    grad = grad + grads_in[j, i, 0].astype(f32)
                if final:
                    (send if j % 2 else keep)[slot, j // 2, i] = grad.astype(bf16)
                else:
                    outs[0][j, i, 0] = grad.astype(bf16)
        if final:

            @pl.when(step >= 2)
            def _():
                pl.semaphore_wait(free, 1)

            swap_copy(slot).start()

    if final:

        @pl.when(step >= 1)
        def _():
            swap_copy(before).wait()
            for j in range(2):
                outs[j][:, 0] = (
                    keep[before, j].astype(f32) + got[before, j].astype(f32)
                ).astype(bf16)

            @pl.when(step <= count - 2)
            def _():
                pl.semaphore_signal(
                    free, inc=1, device_id=partner, device_id_type=pl.DeviceIdType.MESH
                )


def moe_call(ident, base, h, g, coef, weights, sums, grads, final):
    tokens, width = h.shape
    hidden = weights[0].shape[3]
    chunk = width // 4
    first, partial = sums is None, grads is not None

    def whole(shape):
        return pl.BlockSpec(shape, lambda i: (0,) * len(shape), pipeline_mode=pl.Buffered(1))

    def expert_block(lead):
        at = (lambda i: jnp.minimum(i, GROUP - 1)) if lead else (lambda i: jnp.maximum(i - 1, 0))
        shape = (*lead, 3, 1, hidden, chunk)
        return pl.BlockSpec(shape, lambda i: (0,) * len(lead) + (0, at(i), 0, 0))

    totals = [jax.ShapeDtypeStruct(a.shape, f32) for a in (h, h, coef)]
    scratch = [pltpu.VMEM((2, 3, width, hidden), bf16), pltpu.SemaphoreType.DMA((2, 4))]
    if final:
        scratch += [pltpu.VMEM((2, 2, 3, hidden, chunk), bf16)] * 3
        scratch += [pltpu.SemaphoreType.DMA((2,))] * 2 + [pltpu.SemaphoreType.REGULAR]
    lead = () if final else (4,)
    grad_shape = jax.ShapeDtypeStruct((*lead, 3, GROUP, hidden, chunk), bf16)
    extra = ({} if not final else {"collective_id": ident, "has_side_effects": True})
    return pl.pallas_call(
        functools.partial(moe_kernel, first, partial, final, base, GROUP),
        grid=(GROUP + 1 if final else GROUP,),
        in_specs=[whole(a.shape) for a in (h, g, coef)]
        + [pl.BlockSpec(memory_space=pl.ANY)] * 4
        + ([] if first else [whole(a.shape) for a in sums])
        + ([expert_block((4,))] if partial else []),
        out_specs=[whole(a.shape) for a in totals] + [expert_block(lead)] * (2 if final else 1),
        scratch_shapes=scratch,
        out_shape=totals + [grad_shape] * (2 if final else 1),
        compiler_params=pltpu.CompilerParams(
            dimension_semantics=("arbitrary",), vmem_limit_bytes=60 * 1024 * 1024, **extra
        ),
        cost_estimate=pl.CostEstimate(
            flops=18 * tokens * width * hidden * GROUP,
            bytes_accessed=12 * width * hidden * GROUP + 32 * tokens * width,
            transcendentals=GROUP * tokens * hidden,
        ),
    )(h, g, coef, *weights, *(() if first else sums), *((grads,) if partial else ()))


def finish_kernel(count, more, places, own_ref, *refs):
    gate_ref, up_ref, down_ref = refs[-3:]

    def put(ref):
        gate_ref[0] = ref[0, 0].astype(f32).T
        up_ref[0] = ref[1, 0].astype(f32).T
        down_ref[0] = ref[2, 0].astype(f32)

    pl.when(pl.program_id(0) < count)(lambda: put(own_ref))
    if more:
        pl.when(pl.program_id(0) >= count)(lambda: put(refs[0]))


def finish_call(places, experts, own, other, grads):
    count, hidden, chunk = own.shape[1:]
    first = grads is None
    shapes = [(experts, chunk, hidden), (experts, chunk, hidden), (experts, hidden, chunk)]
    pieces = [pl.BlockSpec((3, 1, hidden, chunk), lambda i, p: (0, jnp.minimum(i, count - 1), 0, 0))]
    if other is not None:
        pieces.append(
            pl.BlockSpec((3, 1, hidden, chunk), lambda i, p: (0, jnp.maximum(i - count, 0), 0, 0))
        )
    old = 1 + len(pieces)
    return pl.pallas_call(
        functools.partial(finish_kernel, count, other is not None),
        grid_spec=pltpu.PrefetchScalarGridSpec(
            num_scalar_prefetch=1,
            grid=(count * len(pieces),),
            in_specs=pieces + ([] if first else [pl.BlockSpec(memory_space=pl.ANY)] * 3),
            out_specs=[pl.BlockSpec((1, *s[1:]), lambda i, p: (p[i], 0, 0)) for s in shapes],
        ),
        out_shape=[jax.ShapeDtypeStruct(s, f32) for s in shapes],
        input_output_aliases={} if first else {old: 0, old + 1: 1, old + 2: 2},
        compiler_params=pltpu.CompilerParams(
            dimension_semantics=("arbitrary",), vmem_limit_bytes=24 * 1024 * 1024
        ),
        cost_estimate=pl.CostEstimate(
            flops=0, bytes_accessed=36 * count * chunk * hidden, transcendentals=0
        ),
        name="finish",
    )(places, own, *(() if other is None else (other,)), *(() if first else grads))


def qkv_kernel(x_ref, gain_ref, w0, w1, w2, w3, proj_ref, h_ref, rate_ref, sq_ref, sq_acc):
    step = pl.program_id(0)

    @pl.when(step == 0)
    def _():
        x = x_ref[...].astype(f32)
        rate = lax.rsqrt(jnp.mean(x * x, axis=-1, keepdims=True) + EPSILON)
        rate_ref[...] = rate
        h_ref[...] = (x * rate * gain_ref[...]).astype(bf16)
        sq_acc[...] = jnp.zeros_like(sq_acc)

    chunk = w0.shape[0]
    proj = sum(nn(h_ref[:, j * chunk : (j + 1) * chunk], w[...]) for j, w in enumerate((w0, w1, w2, w3)))
    proj_ref[...] = proj
    lanes = lax.broadcasted_iota(jnp.int32, sq_acc.shape, 1)
    sq_acc[...] += jnp.where(lanes == step, jnp.sum(proj * proj, axis=-1, keepdims=True), 0.0)

    @pl.when(step == 2)
    def _():
        sq_ref[...] = sq_acc[...].T[: sq_ref.shape[0]]


def qkv_call(x, gain, weights):
    tokens, width = x.shape
    chunk, cols = weights[0].shape[0], weights[0].shape[1] // 3
    return pl.pallas_call(
        qkv_kernel,
        grid=(3,),
        in_specs=[
            pl.BlockSpec((tokens, width), lambda i: (0, 0), pipeline_mode=pl.Buffered(1)),
            pl.BlockSpec((1, width), lambda i: (0, 0)),
        ]
        + [pl.BlockSpec((chunk, cols), lambda i: (0, i))] * 4,
        out_specs=[
            pl.BlockSpec((tokens, cols), lambda i: (0, i)),
            pl.BlockSpec((tokens, width), lambda i: (0, 0)),
            pl.BlockSpec((tokens, 1), lambda i: (0, 0)),
            pl.BlockSpec((8, tokens), lambda i: (0, 0)),
        ],
        scratch_shapes=[pltpu.VMEM((tokens, 128), f32)],
        out_shape=[
            jax.ShapeDtypeStruct((tokens, 3 * cols), f32),
            jax.ShapeDtypeStruct((tokens, width), bf16),
            jax.ShapeDtypeStruct((tokens, 1), f32),
            jax.ShapeDtypeStruct((8, tokens), f32),
        ],
        compiler_params=pltpu.CompilerParams(
            dimension_semantics=("arbitrary",), vmem_limit_bytes=40 * 1024 * 1024
        ),
        cost_estimate=pl.CostEstimate(
            flops=6 * tokens * width * cols, bytes_accessed=12 * width * cols, transcendentals=tokens
        ),
        name="qkv",
    )(x, gain[None], *weights)


def meet(peers):
    barrier = pltpu.get_barrier_semaphore()
    for here, place in peers:

        @pl.when(here)
        def _(place=place):
            pl.semaphore_signal(
                barrier, inc=1, device_id={"tensor": place}, device_id_type=pl.DeviceIdType.MESH
            )

    pl.semaphore_wait(barrier, sum(here.astype(jnp.int32) for here, _ in peers))


def line_kernel(n, subs, streams, *refs):
    refs = list(refs)
    ins = [[refs.pop(0) for _ in range(1 + extra)] for _, extra, _ in streams]
    outs = [[refs.pop(0) for _ in range(1 + more)] for _, _, more in streams]
    scratch = [[refs.pop(0) for _ in range(3)] for _ in streams]
    z = lax.axis_index("tensor")
    inner = (z > 0, z < n - 1)
    side = (z - 1, z + 1)
    meet([(inner[0], z - 1), (inner[1], z + 1)])

    class Stream:
        def __init__(self, finish, part_ref, extras, out_ref, more, buf, total, sems):
            self.finish, self.part, self.extras, self.out = finish, part_ref, extras, out_ref
            self.more, self.buf, self.total, self.sems = more, buf, total, sems
            self.block = part_ref.shape[0] // n
            self.size = self.block // subs

        def rows(self, b, s):
            return pl.ds(pl.multiple_of(b * self.block + s * self.size, self.size), self.size)

        def copy(self, kind, way, b, s):
            at = self.rows(b, s)
            return pltpu.make_async_remote_copy(
                src_ref=self.out.at[at] if kind else self.buf.at[way, 0, at],
                dst_ref=self.out.at[at] if kind else self.buf.at[way, 1, at],
                send_sem=self.sems.at[2 * kind, way, b, s],
                recv_sem=self.sems.at[2 * kind + 1, way, b, s],
                device_id={"tensor": side[way]},
                device_id_type=pl.DeviceIdType.MESH,
            )

        def open(self, way):
            @pl.when(jnp.logical_not(inner[1 - way]))
            def _():
                for s in range(subs):
                    for i in range(1, n):
                        b = n - i if way else i - 1
                        self.buf[way, 0, self.rows(b, s)] = self.part[self.rows(b, s)]
                        self.copy(0, way, b, s).start()

        def pass_on(self, way, b, s):
            @pl.when(inner[1 - way] & ((z < b) if way else (z > b)))
            def _():
                at = self.rows(b, s)
                self.copy(0, way, b, s).wait_recv()
                mine = self.part[at].astype(f32)
                self.buf[way, 0, at] = (mine + self.buf[way, 1, at].astype(f32)).astype(bf16)
                self.copy(0, way, b, s).start()

        def own(self, s):
            at = self.rows(z, s)
            self.total[...] = self.part[at].astype(f32)
            for way in (0, 1):

                @pl.when(inner[1 - way])
                def _(way=way):
                    self.copy(0, way, z, s).wait_recv()
                    self.total[...] += self.buf[way, 1, at].astype(f32)

            local = pl.ds(s * self.size, self.size)
            self.out[at] = self.finish(s, self.total[...], at, local, self.extras, self.more)
            for way in (0, 1):

                @pl.when(inner[way])
                def _(way=way):
                    self.copy(1, way, z, s).start()

        def forward(self, d, s):
            for way in (0, 1):
                b = z - d if way else z + d

                @pl.when(inner[way] & ((b >= 0) if way else (b <= n - 1)))
                def _(way=way, b=b):
                    self.copy(1, way, b, s).wait_recv()
                    self.copy(1, way, b, s).start()

        def close(self, way, b, s):
            ahead = (z < b) if way else (z > b)
            past = (z > b) if way else (z < b)

            @pl.when(past & jnp.logical_not(inner[way]))
            def _():
                self.copy(1, way, b, s).wait_recv()

            @pl.when(ahead)
            def _():
                self.copy(0, way, b, s).wait_send()

            @pl.when(inner[way] & jnp.logical_not(ahead))
            def _():
                self.copy(1, way, b, s).wait_send()

    flows = [
        Stream(finish, i[0], i[1:], o[0], o[1:], *c)
        for (finish, _, _), i, o, c in zip(streams, ins, outs, scratch)
    ]
    for flow in flows:
        for way in (0, 1):
            flow.open(way)
    for s in range(subs + 1):
        for flow in flows:
            if s < subs:
                for i in range(1, n):
                    flow.pass_on(1, n - i, s)
                    flow.pass_on(0, i - 1, s)
            if s:
                flow.own(s - 1)
                for d in range(1, n - 1):
                    if s - 1 >= d:
                        flow.forward(d, s - 1 - d)
    for s in range(subs):
        for flow in flows:
            for d in range(1, n - 1):
                if s + d >= subs:
                    flow.forward(d, s)
    for flow in flows:
        for s in range(subs):
            for b in range(n):
                for way in (0, 1):
                    flow.close(way, b, s)


def line_call(ident, n, streams):
    subs = 2
    vmem = pl.BlockSpec(memory_space=pltpu.VMEM)
    shapes, scratch, inputs, kinds = [], [], [], []
    for finish, part, extras, more in streams:
        tokens, width = part.shape
        kinds.append((finish, len(extras), len(more)))
        inputs += [part, *extras]
        shapes += [jax.ShapeDtypeStruct((tokens, width), bf16)]
        shapes += [jax.ShapeDtypeStruct(m, f32) for m in more]
        scratch += [
            pltpu.VMEM((2, 2, tokens, width), bf16),
            pltpu.VMEM((tokens // n // subs, width), f32),
            pltpu.SemaphoreType.DMA((4, 2, n, subs)),
        ]
    return pl.pallas_call(
        functools.partial(line_kernel, n, subs, kinds),
        in_specs=[vmem] * len(inputs),
        out_specs=[vmem] * len(shapes),
        out_shape=shapes,
        scratch_shapes=scratch,
        compiler_params=pltpu.CompilerParams(
            collective_id=ident, has_side_effects=True, vmem_limit_bytes=58 * 1024 * 1024
        ),
        cost_estimate=pl.CostEstimate(
            flops=12000 * tokens * width, bytes_accessed=8 * tokens * width, transcendentals=0
        ),
    )(*inputs)


def after_attention(s, total, whole, local, refs, more):
    x_ref, gain_ref = refs
    y_ref, rate_ref = more
    y = x_ref[whole].astype(f32) + total
    rate = lax.rsqrt(jnp.mean(y * y, axis=-1, keepdims=True) + EPSILON)
    y_ref[local] = y
    rate_ref[local] = rate
    return (y * rate * gain_ref[...]).astype(bf16)


def norm_back(total, base, x, rate, gain_ref, grad_ref, s):
    terms = jnp.sum(total * (x * rate), axis=0, keepdims=True)
    grad_ref[...] = terms if s == 0 else grad_ref[...] + terms
    e = total * gain_ref[...]
    return base + rate * e - x * (rate * rate * rate) * jnp.mean(e * x, axis=-1, keepdims=True)


def after_experts(s, total, whole, local, refs, more):
    g_ref, y_ref, rate_ref, gain_ref = refs
    dy_ref, grad_ref = more
    dy = norm_back(
        total, g_ref[whole].astype(f32), y_ref[local], rate_ref[local], gain_ref, grad_ref, s
    )
    dy_ref[local] = dy
    return dy.astype(bf16)


def after_projections(s, total, whole, local, refs, more):
    x_ref, dy_ref, rate_ref, gain_ref = refs
    (grad_ref,) = more
    x = x_ref[whole].astype(f32)
    dx = norm_back(total, dy_ref[local], x, rate_ref[whole], gain_ref, grad_ref, s)
    return dx.astype(bf16)


def block_rows(s, total, whole, local, refs, more):
    y_ref, valid_ref = refs
    return (valid_ref[whole] * (y_ref[local] + total)).astype(bf16)


def exchange(n, mine_ref, got_ref, sems):
    z = lax.axis_index("tensor")
    places = [lax.rem(z + d, n) for d in range(n)]
    meet([(z >= 0, p) for p in places[1:]])
    copies = [
        pltpu.make_async_remote_copy(
            src_ref=mine_ref,
            dst_ref=got_ref.at[z],
            send_sem=sems.at[0, d],
            recv_sem=sems.at[1, d],
            device_id={"tensor": places[d]},
            device_id_type=pl.DeviceIdType.MESH,
        )
        for d in range(1, n)
    ]
    for c in copies:
        c.start()
    got_ref[z] = mine_ref[...]

    def total():
        for c in copies:
            c.wait()
        return sum(got_ref[i] for i in range(n))

    return total


def rope_kernel(n, proj_ref, sq_ref, gq_ref, gk_ref, cos_ref, sin_ref, q_ref, kv_ref, rate_ref, mine, got, sems):
    _, cols = q_ref.shape
    mine[...] = sq_ref[...]
    total = exchange(n, mine, got, sems)
    kv_ref[:, cols:] = proj_ref[:, 2 * cols :].astype(bf16)
    sums = total()
    rates = lax.rsqrt(sums / (n * cols) + EPSILON).T
    rate_ref[...] = rates
    cosine, sine = cos_ref[...], sin_ref[...]

    def turned(part, rate, gain, head):
        at = slice(head * HEAD_DIM, (head + 1) * HEAD_DIM)
        a = proj_ref[:, part * cols + head * HEAD_DIM : part * cols + (head + 1) * HEAD_DIM]
        a = a * rate * gain[:, at]
        return (a * cosine + pltpu.roll(a, HEAD_DIM // 2, 1) * sine).astype(bf16)

    for head in range(cols // HEAD_DIM):
        at = slice(head * HEAD_DIM, (head + 1) * HEAD_DIM)
        q_ref[:, at] = turned(0, rates[:, 0:1], gq_ref, head)
        kv_ref[:, at] = turned(1, rates[:, 1:2], gk_ref, head)


def exchange_scratch(n, tokens, rows=8):
    return [
        pltpu.VMEM((rows, tokens), f32),
        pltpu.VMEM((n, rows, tokens), f32),
        pltpu.SemaphoreType.DMA((2, n)),
    ]


def rope_call(n, proj, sq, gq, gk, cosine, sine):
    tokens, cols = proj.shape[0], proj.shape[1] // 3
    vmem = pl.BlockSpec(memory_space=pltpu.VMEM)
    return pl.pallas_call(
        functools.partial(rope_kernel, n),
        in_specs=[vmem] * 6,
        out_specs=[vmem] * 3,
        out_shape=[
            jax.ShapeDtypeStruct((tokens, cols), bf16),
            jax.ShapeDtypeStruct((tokens, 2 * cols), bf16),
            jax.ShapeDtypeStruct((tokens, 8), f32),
        ],
        scratch_shapes=exchange_scratch(n, tokens),
        compiler_params=pltpu.CompilerParams(
            collective_id=1, has_side_effects=True, vmem_limit_bytes=40 * 1024 * 1024
        ),
        cost_estimate=pl.CostEstimate(
            flops=2000 * tokens * cols, bytes_accessed=18 * tokens * cols, transcendentals=tokens
        ),
        name="rope",
    )(proj, sq, gq[None], gk[None], cosine, sine)


def qk_back_kernel(
    n, dq_ref, dk_ref, dv_ref, far_ref, proj_ref, rate_ref, gq_ref, gk_ref, cos_ref, sin_ref, dc_ref,
    out_ref, grad_ref, dcs_ref, dn, mine, got, sems,
):
    tokens, cols = dq_ref.shape
    cosine, sine = cos_ref[...], sin_ref[...]
    lanes = lax.broadcasted_iota(jnp.int32, (tokens, HEAD_DIM), 1)
    stats = jnp.zeros((tokens, HEAD_DIM), f32)
    rates = rate_ref[...]
    for part, gain in ((0, gq_ref), (1, gk_ref)):
        stat = jnp.zeros((tokens, 1), f32)
        rate = rates[:, part : part + 1]
        for head in range(cols // HEAD_DIM):
            at = slice(head * HEAD_DIM, (head + 1) * HEAD_DIM)
            if part:
                a = dk_ref[:, at] + far_ref[:, at].astype(f32)
            else:
                a = dq_ref[:, at]
            a = a * cosine - pltpu.roll(a, HEAD_DIM // 2, 1) * sine
            plain = proj_ref[:, part * cols + head * HEAD_DIM : part * cols + (head + 1) * HEAD_DIM]
            grad_ref[part : part + 1, at] = jnp.sum(a * plain * rate, axis=0, keepdims=True)
            a = a * gain[:, at]
            dn[part, :, at] = a
            stat += jnp.sum(a * plain, axis=-1, keepdims=True)
        stats = jnp.where(lanes == part, stat, stats)
    mine[:8] = stats.T[:8]
    mine[8:] = dc_ref[...]
    total = exchange(n, mine, got, sems)
    out_ref[:, 2 * cols :] = (dv_ref[...] + far_ref[:, cols:].astype(f32)).astype(bf16)
    whole = total()
    dcs_ref[...] = whole[8:]
    means = (whole[:8] / (n * cols)).T
    for part in (0, 1):
        rate = rates[:, part : part + 1]
        factor = rate * rate * rate * means[:, part : part + 1]
        at = slice(part * cols, (part + 1) * cols)
        out_ref[:, at] = (rate * dn[part] - proj_ref[:, at] * factor).astype(bf16)


def qk_back_call(n, dq, dk, dv, far, proj, rates, gq, gk, cosine, sine, dcoef):
    tokens, cols = dq.shape
    vmem = pl.BlockSpec(memory_space=pltpu.VMEM)
    near = pl.BlockSpec((tokens, cols), lambda i: (0, 0))
    return pl.pallas_call(
        functools.partial(qk_back_kernel, n),
        grid=(1,),
        in_specs=[vmem, near, near] + [vmem] * 8,
        out_specs=[vmem] * 3,
        out_shape=[
            jax.ShapeDtypeStruct((tokens, 3 * cols), bf16),
            jax.ShapeDtypeStruct((8, cols), f32),
            jax.ShapeDtypeStruct(dcoef.shape, f32),
        ],
        scratch_shapes=[pltpu.VMEM((2, tokens, cols), f32)]
        + exchange_scratch(n, tokens, 8 + dcoef.shape[0]),
        compiler_params=pltpu.CompilerParams(
            collective_id=2, has_side_effects=True, vmem_limit_bytes=40 * 1024 * 1024
        ),
        cost_estimate=pl.CostEstimate(
            flops=2000 * tokens * cols, bytes_accessed=30 * tokens * cols, transcendentals=0
        ),
        name="qk_back",
    )(dq, dk, dv, far, proj, rates, gq[None], gk[None], cosine, sine, dcoef)


def gains_kernel(sizes, both, in_ref, out_ref, mine, *bufs):
    mine[...] = in_ref[...]
    peers = []
    for axis, n in sizes:
        here = lax.axis_index(axis)
        peers += [(axis, d, lax.rem(here + d, n)) for d in range(1, n)]
    barrier = pltpu.get_barrier_semaphore()
    for axis, _, place in peers:
        pl.semaphore_signal(
            barrier, inc=1, device_id={axis: place}, device_id_type=pl.DeviceIdType.MESH
        )
    pl.semaphore_wait(barrier, len(peers))
    for k, (axis, n) in enumerate(sizes):
        got, sems = bufs[2 * k : 2 * k + 2]
        here = lax.axis_index(axis)
        rows = pl.ds(0, both if axis == "tensor" else mine.shape[0])
        copies = [
            pltpu.make_async_remote_copy(
                src_ref=mine.at[rows],
                dst_ref=got.at[here],
                send_sem=sems.at[0, d],
                recv_sem=sems.at[1, d],
                device_id={axis: place},
                device_id_type=pl.DeviceIdType.MESH,
            )
            for a, d, place in peers
            if a == axis
        ]
        for c in copies:
            c.start()
        got[here] = mine[rows]
        for c in copies:
            c.wait()
        mine[rows] = sum(got[i] for i in range(n))
    out_ref[...] = mine[...]


def gains_call(sizes, both, values):
    rows = values.shape[0]
    vmem = pl.BlockSpec(memory_space=pltpu.VMEM)
    scratch = [pltpu.VMEM((rows, 128), f32)]
    for axis, n in sizes:
        scratch += [
            pltpu.VMEM((n, both if axis == "tensor" else rows, 128), f32),
            pltpu.SemaphoreType.DMA((2, n)),
        ]
    return pl.pallas_call(
        functools.partial(gains_kernel, sizes, both),
        in_specs=[vmem],
        out_specs=vmem,
        out_shape=jax.ShapeDtypeStruct(values.shape, f32),
        scratch_shapes=scratch,
        compiler_params=pltpu.CompilerParams(collective_id=6, has_side_effects=True),
        cost_estimate=pl.CostEstimate(flops=10000000, bytes_accessed=100000, transcendentals=0),
        name="gains",
    )(values)


def grads_kernel(count, *refs):
    pairs = [(refs[2 * i], refs[2 * i + 1]) for i in range(count)]
    out0, out2, send, got, send_sems, got_sems = refs[2 * count :]
    me = lax.axis_index("shard")
    partner = {"shard": me + 1 - 2 * lax.rem(me, 2)}
    chunk = send.shape[1]
    barrier = pltpu.get_barrier_semaphore()
    pl.semaphore_signal(barrier, inc=1, device_id=partner, device_id_type=pl.DeviceIdType.MESH)
    pl.semaphore_wait(barrier, 1)

    def products(j, put):
        col = 0
        for left, right in pairs:
            n = right.shape[1]
            put(slice(col, col + n), tn(left[:, j * chunk : (j + 1) * chunk], right[...]))
            col += n

    copies = []
    for k, j in enumerate((1, 3)):

        def store(at, value, k=k):
            send[k, :, at] = value.astype(bf16)

        products(j, store)
        copies.append(
            pltpu.make_async_remote_copy(
                src_ref=send.at[k],
                dst_ref=got.at[k],
                send_sem=send_sems.at[k],
                recv_sem=got_sems.at[k],
                device_id=partner,
                device_id_type=pl.DeviceIdType.MESH,
            )
        )
        copies[k].start()
    for k, (j, out) in enumerate(((0, out0), (2, out2))):
        copies[k].wait_recv()

        def store(at, value, k=k, out=out):
            out[:, at] = (value + got[k, :, at].astype(f32)).astype(bf16)

        products(j, store)
    for c in copies:
        c.wait_send()


def grads_call(ident, pairs):
    tokens, width = pairs[0][0].shape
    chunk, cols = width // 4, sum(b.shape[1] for _, b in pairs)
    vmem = pl.BlockSpec(memory_space=pltpu.VMEM)
    return pl.pallas_call(
        functools.partial(grads_kernel, len(pairs)),
        in_specs=[vmem] * (2 * len(pairs)),
        out_specs=[vmem] * 2,
        out_shape=[jax.ShapeDtypeStruct((chunk, cols), bf16)] * 2,
        scratch_shapes=[pltpu.VMEM((2, chunk, cols), bf16)] * 2 + [pltpu.SemaphoreType.DMA((2,))] * 2,
        compiler_params=pltpu.CompilerParams(
            collective_id=ident, has_side_effects=True, vmem_limit_bytes=50 * 1024 * 1024
        ),
        cost_estimate=pl.CostEstimate(
            flops=2 * tokens * width * cols, bytes_accessed=4 * tokens * width, transcendentals=0
        ),
    )(*(a for p in pairs for a in p))


def masked_scores(base, q, keys, scale, flip):
    tokens = q.shape[0]
    raw = (nt(keys, q) if flip else nt(q, keys)) * scale
    axis = 0 if flip else 1
    parts = []
    for i in range(keys.shape[0] // tokens):
        rows = slice(i * tokens, (i + 1) * tokens)
        part = raw[rows] if flip else raw[:, rows]
        key_pos = base[i + 1] + lax.broadcasted_iota(jnp.int32, part.shape, axis)
        query_pos = base[0] + lax.broadcasted_iota(jnp.int32, part.shape, 1 - axis)
        parts.append(jnp.where(key_pos <= query_pos, part, -1e30))
    return jnp.concatenate(parts, axis=axis)


def attention_kernel(scale, base, q_ref, k_ref, v_ref, w0, w1, w2, w3, mixed_ref, lse_ref, part_ref, lse_acc):
    head = pl.program_id(0)
    scores = masked_scores(base, q_ref[...], k_ref[...], scale, False)
    top = jnp.max(scores, axis=-1, keepdims=True)
    expo = jnp.exp(scores - top)
    total = jnp.sum(expo, axis=-1, keepdims=True)
    mixed = nn((expo / total).astype(bf16), v_ref[...]).astype(bf16)
    for h in range(mixed_ref.shape[1] // HEAD_DIM):

        @pl.when(head == h)
        def _(h=h):
            mixed_ref[:, h * HEAD_DIM : (h + 1) * HEAD_DIM] = mixed

    @pl.when(head == 0)
    def _():
        lse_acc[...] = jnp.zeros_like(lse_acc)

    lanes = lax.broadcasted_iota(jnp.int32, lse_acc.shape, 1)
    lse_acc[...] += jnp.where(lanes == head, top + jnp.log(total), 0.0)

    @pl.when(head == pl.num_programs(0) - 1)
    def _():
        lse_ref[...] = lse_acc[...].T[: lse_ref.shape[0]]
        chunk = w0.shape[0]
        for j, w in enumerate((w0, w1, w2, w3)):
            part_ref[:, j * chunk : (j + 1) * chunk] = nt(mixed_ref[...], w[...]).astype(bf16)


def attention_call(base, q, kv, weights, scale):
    tokens, cols = q.shape
    heads, keys, chunk = cols // HEAD_DIM, kv.shape[0], weights[0].shape[0]
    return pl.pallas_call(
        functools.partial(attention_kernel, scale),
        grid_spec=pltpu.PrefetchScalarGridSpec(
            num_scalar_prefetch=1,
            grid=(heads,),
            in_specs=[
                pl.BlockSpec((tokens, HEAD_DIM), lambda h, b: (0, h)),
                pl.BlockSpec((keys, HEAD_DIM), lambda h, b: (0, h)),
                pl.BlockSpec((keys, HEAD_DIM), lambda h, b: (0, heads + h)),
            ]
            + [pl.BlockSpec((chunk, cols), lambda h, b: (0, 0), pipeline_mode=pl.Buffered(1))] * 4,
            out_specs=[
                pl.BlockSpec((tokens, cols), lambda h, b: (0, 0)),
                pl.BlockSpec((8, tokens), lambda h, b: (0, 0)),
                pl.BlockSpec((tokens, 4 * chunk), lambda h, b: (0, 0)),
            ],
            scratch_shapes=[pltpu.VMEM((tokens, 128), f32)],
        ),
        out_shape=[
            jax.ShapeDtypeStruct((tokens, cols), bf16),
            jax.ShapeDtypeStruct((8, tokens), f32),
            jax.ShapeDtypeStruct((tokens, 4 * chunk), bf16),
        ],
        compiler_params=pltpu.CompilerParams(
            dimension_semantics=("arbitrary",), vmem_limit_bytes=50 * 1024 * 1024
        ),
        cost_estimate=pl.CostEstimate(
            flops=4 * tokens * keys * cols * 4 + 8 * tokens * cols * chunk,
            bytes_accessed=8 * tokens * cols,
            transcendentals=heads * tokens * keys,
        ),
        name="attention",
    )(base, q, kv, kv, *weights)


def attention_back_kernel(
    scale, base, da_ref, q_ref, k_ref, v_ref, lse_ref, w0, w1, w2, w3, dq_ref, dk_ref, dv_ref, dmix
):
    head = pl.program_id(0)

    @pl.when(head == 0)
    def _():
        chunk = w0.shape[0]
        whole = sum(
            nn(da_ref[:, j * chunk : (j + 1) * chunk], w[...])
            for j, w in enumerate((w0, w1, w2, w3))
        ).astype(bf16)
        for h in range(dmix.shape[0]):
            dmix[h] = whole[:, h * HEAD_DIM : (h + 1) * HEAD_DIM]

    q, keys, values, dm = q_ref[...], k_ref[...], v_ref[...], dmix[head]
    scores = masked_scores(base, q, keys, scale, True)
    probs = jnp.exp(scores - lse_ref[pl.ds(head, 1), :])
    dprobs = nt(values, dm)
    ds = (probs * (dprobs - jnp.sum(probs * dprobs, axis=0, keepdims=True))).astype(bf16)
    dq_ref[...] = tn(ds, keys) * scale
    dk_ref[...] = nn(ds, q) * scale
    dv_ref[...] = nn(probs.astype(bf16), dm)


def attention_back_call(base, da, q, kv, lse, weights, scale):
    tokens, cols = q.shape
    heads, keys, chunk = cols // HEAD_DIM, kv.shape[0], weights[0].shape[0]
    return pl.pallas_call(
        functools.partial(attention_back_kernel, scale),
        grid_spec=pltpu.PrefetchScalarGridSpec(
            num_scalar_prefetch=1,
            grid=(heads,),
            in_specs=[
                pl.BlockSpec(da.shape, lambda h, b: (0, 0), pipeline_mode=pl.Buffered(1)),
                pl.BlockSpec((tokens, HEAD_DIM), lambda h, b: (0, h)),
                pl.BlockSpec((keys, HEAD_DIM), lambda h, b: (0, h)),
                pl.BlockSpec((keys, HEAD_DIM), lambda h, b: (0, heads + h)),
                pl.BlockSpec(lse.shape, lambda h, b: (0, 0)),
            ]
            + [pl.BlockSpec((chunk, cols), lambda h, b: (0, 0), pipeline_mode=pl.Buffered(1))] * 4,
            out_specs=[
                pl.BlockSpec((tokens, HEAD_DIM), lambda h, b: (0, h)),
                pl.BlockSpec((keys, HEAD_DIM), lambda h, b: (0, h)),
                pl.BlockSpec((keys, HEAD_DIM), lambda h, b: (0, h)),
            ],
            scratch_shapes=[pltpu.VMEM((heads, tokens, HEAD_DIM), bf16)],
        ),
        out_shape=[
            jax.ShapeDtypeStruct((tokens, cols), f32),
            jax.ShapeDtypeStruct((keys, cols), f32),
            jax.ShapeDtypeStruct((keys, cols), f32),
        ],
        compiler_params=pltpu.CompilerParams(
            dimension_semantics=("arbitrary",), vmem_limit_bytes=50 * 1024 * 1024
        ),
        cost_estimate=pl.CostEstimate(
            flops=10 * tokens * keys * cols + 8 * tokens * cols * chunk,
            bytes_accessed=24 * tokens * cols,
            transcendentals=heads * tokens * keys,
        ),
        name="attention_back",
    )(base, da, q, kv, kv, lse, *weights)


def body(
    hidden, norm1_gain, w_query, w_key, w_value, query_gain, key_gain, w_output,
    norm2_gain, w_router, w_gate, w_up, w_down, seq_lengths, expert_routes, out_grad,
):
    slots, tokens, width = hidden.shape
    shards, contexts, tensors = (
        lax.axis_size("shard"),
        lax.axis_size("context"),
        lax.axis_size("tensor"),
    )
    assert slots == 1 and shards == 4
    me, here = lax.axis_index("shard"), lax.axis_index("context")
    pair = contexts == 2
    chunk = width // shards
    cols = w_query.shape[1]
    experts = w_gate.shape[0]
    scale = HEAD_DIM ** (-0.5)
    rows = tokens // tensors

    def to_core(a):
        return lax.ppermute(a, "shard", [(s, s ^ 1) for s in range(shards)])

    def to_x(a):
        return lax.ppermute(a, "shard", [(s, s ^ 2) for s in range(shards)])

    def to_y(a):
        return lax.ppermute(a, "context", [(0, 1), (1, 0)])

    def turn(a, axis):
        return jnp.concatenate(
            [
                lax.dynamic_slice_in_dim(a, jnp.bitwise_xor(me, j) * chunk, chunk, axis)
                for j in range(shards)
            ],
            axis=axis,
        )

    def around(a):
        return lax.psum(a.astype(f32), "context") - a.astype(f32)

    qkv_own = jnp.concatenate([w_query, w_key, w_value], axis=1)
    qkv_x = to_x(qkv_own)
    qkv = [qkv_own, to_core(qkv_own), qkv_x, to_core(qkv_x)]
    out_own = jnp.concatenate(
        [w_output.T, jnp.pad(w_router, ((0, 0), (0, 128 - experts)))], axis=1
    )
    out_x = to_x(out_own)
    outs = [out_own, to_core(out_own), out_x, to_core(out_x)]
    local = experts // contexts if pair else experts
    offset = here * local if pair else 0

    def mine_of(w):
        return lax.dynamic_slice_in_dim(w, offset, local, 0)

    w_own = jnp.stack([mine_of(w_gate), mine_of(w_up), mine_of(w_down).transpose(0, 2, 1)])
    w_core = to_core(w_own)
    groups = local // GROUP
    fetched = []
    for n in range(groups):
        w_x = to_x(w_own[:, n * GROUP : (n + 1) * GROUP])
        fetched.append((w_own, w_core, w_x, to_core(w_x)))

    x_low = turn(hidden.reshape(tokens, width), 1)
    g_low = turn(out_grad.reshape(tokens, width), 1)
    gain1, gain2 = turn(norm1_gain, 0), turn(norm2_gain, 0)
    positions = here * tokens + jnp.arange(tokens, dtype=jnp.int32)
    valid = (positions < seq_lengths[0]).astype(f32)[:, None]
    g_all = (g_low.astype(f32) * valid).astype(bf16)
    routes = expert_routes.reshape(tokens, expert_routes.shape[-1])
    member = jnp.any(
        routes[:, :, None] == jnp.arange(experts, dtype=jnp.int32)[None, None, :], axis=1
    ).astype(f32)
    if pair:
        g_far = to_y(
            jnp.concatenate([g_all, jnp.pad(member, ((0, 0), (0, 128 - experts))).astype(bf16)], axis=1),
        )
        g_far, member_far = g_far[:, :width], g_far[:, width : width + experts].astype(f32)
    proj, h1, rate1, squares = qkv_call(x_low, gain1, qkv)
    inv_freq = 10000.0 ** (-(2.0 * jnp.arange(HEAD_DIM // 2, dtype=f32)) / HEAD_DIM)
    angles = positions.astype(f32)[:, None] * inv_freq[None, :]
    cosine, sine = jnp.cos(angles), jnp.sin(angles)
    cosine = jnp.concatenate([cosine, cosine], axis=1)
    sine = jnp.concatenate([-sine, sine], axis=1)
    q_rot, kv, rates = rope_call(tensors, proj, squares, query_gain, key_gain, cosine, sine)
    if pair:
        kv_all = jnp.concatenate([kv, to_y(kv)], axis=0)
        base = jnp.stack([here, here, 1 - here])
    else:
        kv_all = lax.all_gather(kv, "context", axis=0, tiled=True)
        base = jnp.concatenate([here[None], jnp.arange(contexts)])
    base = (base * tokens).astype(jnp.int32)
    w_outs = [o[:, :cols] for o in outs]
    mixed, lse, attn_part = attention_call(base, q_rot, kv_all, w_outs, scale)
    w_rout = jnp.concatenate([o[:, cols : cols + experts] for o in outs], axis=0)
    h2, y1, rate2 = line_call(
        3, tensors,
        [(after_attention, attn_part, (x_low, gain2[None]), ((rows, width), (rows, 1)))],
    )

    def route(h, member):
        logits = nn(h, w_rout)
        expo_logit = jnp.exp(logits - jnp.max(logits, axis=-1, keepdims=True))
        router = expo_logit / jnp.sum(expo_logit, axis=-1, keepdims=True)
        return router, lax.dynamic_slice_in_dim(router * member, offset, local, 1)

    router, coef = route(h2, member)
    sums = dict.fromkeys(("own", "far"))
    data = {"own": (h2, g_all, coef)}
    if pair:
        h2_far = to_y(h2)
        data["far"] = (h2_far, g_far, route(h2_far, member_far)[1])
        order = [(n, t) for n in range(groups) for t in (("far", "own") if n else ("own", "far"))]
    else:
        order = [(n, "own") for n in range(groups)]
    grads, partials = None, {}
    for k, (n, t) in enumerate(order):
        final = not pair or n in partials
        done = moe_call(10 + k, n * GROUP, *data[t], fetched[n], sums[t], partials.get(n), final)
        sums[t] = done[:3]
        if not final:
            partials[n] = done[3]
            continue
        near, far = done[3], to_x(done[4])
        cuts = 2 if pair and n == 0 else 1
        for c in range(cuts):
            size = GROUP // cuts
            some = slice(c * size, (c + 1) * size)
            owned = (near[:, some].astype(f32) + far[:, some].astype(f32)).astype(bf16)
            places = offset + n * GROUP + c * size + jnp.arange(size, dtype=jnp.int32)
            if pair:
                other = to_y(owned)
                places = jnp.concatenate([places, places + local - 2 * offset])
            else:
                owned, other = lax.psum(owned.astype(f32), "context").astype(bf16), None
            grads = finish_call(places, experts, owned, other, grads)
    grad_gate, grad_up, grad_down = grads
    moe, dh, dcoef = sums["own"]
    if pair:
        moe_far, dh_far, dcoef_far = sums["far"]
        back = to_y(
            jnp.concatenate(
                [dh_far, jnp.pad(dcoef_far, ((0, 0), (0, 128 - local)))], axis=1
            ).astype(bf16),
        ).astype(f32)
        dh = dh + back[:, :width]
        far_part = back[:, width : width + local]
        dcoef = jnp.where(
            here == 0,
            jnp.concatenate([dcoef, far_part], axis=1),
            jnp.concatenate([far_part, dcoef], axis=1),
        )
        moe = moe + to_y(moe_far.astype(bf16)).astype(f32)

    def route_back(dcoef):
        dprob = dcoef * member
        return (router * (dprob - jnp.sum(router * dprob, axis=-1, keepdims=True))).astype(bf16)

    dlog = route_back(dcoef)
    dh_part = (dh + nt(dlog, w_rout)).astype(bf16)
    da, dy1, gain2_grad = line_call(
        4, tensors,
        [(after_experts, dh_part, (g_all, y1, rate2, gain2[None]), ((rows, width), (1, width)))],
    )

    def chunks_to_owner(ident, pairs):
        near = grads_call(ident, pairs)
        owned = (near[0].astype(f32) + to_x(near[1]).astype(f32)).astype(bf16)
        other = to_y(owned) if pair else around(owned)
        return owned.astype(f32) + other.astype(f32)

    sum_out = chunks_to_owner(7, [(da, mixed)])

    dqr, dkr, dvb = attention_back_call(base, da, q_rot, kv_all, lse, w_outs, scale)
    if pair:
        far = jnp.concatenate([dkr[tokens:], dvb[tokens:]], axis=1).astype(bf16)
        far = to_y(far)
    else:
        dkr, dvb = (
            lax.psum_scatter(a, "context", scatter_dimension=0, tiled=True) for a in (dkr, dvb)
        )
        far = jnp.zeros((tokens, 2 * cols), bf16)
    dqkv, gains_qk, dcoef = qk_back_call(
        tensors, dqr, dkr, dvb, far, proj, rates, query_gain, key_gain, cosine, sine, dcoef.T
    )
    dlog = jnp.pad(route_back(dcoef.T), ((0, 0), (0, 128 - experts)))
    sum_qkv = chunks_to_owner(8, [(h1, dqkv), (h2, dlog)])

    dh1_part = nt(dqkv, jnp.concatenate(qkv, axis=0)).astype(bf16)
    dx, gain1_grad, block = line_call(
        5, tensors,
        [
            (after_projections, dh1_part, (x_low, dy1, rate1, gain1[None]), ((1, width),)),
            (block_rows, moe.astype(bf16), (y1, valid), ()),
        ],
    )
    gain1_grad, gain2_grad = gain1_grad[0], gain2_grad[0]
    input_grad = turn(dx, 1).reshape(hidden.shape)
    block_out = turn(block, 1).reshape(hidden.shape)

    values = jnp.concatenate(
        [turn(gain1_grad, 0), turn(gain2_grad, 0), gains_qk[:2].reshape(-1)]
    ).reshape(-1, 128)
    sizes = (("tensor", tensors), ("shard", shards), ("context", contexts))
    gains = gains_call(sizes, 2 * width // 128, values).reshape(-1)
    gains_qk = gains[2 * width :].reshape(2, cols)
    return (
        block_out,
        input_grad,
        gains[:width],
        sum_qkv[:, :cols],
        sum_qkv[:, cols : 2 * cols],
        sum_qkv[:, 2 * cols : 3 * cols],
        gains_qk[0],
        gains_qk[1],
        sum_out.T,
        gains[width : 2 * width],
        sum_qkv[:, 3 * cols : 3 * cols + experts],
        grad_gate,
        grad_up,
        grad_down,
    )


def solution(mesh):
    in_specs = (
        P("shard", "context", None),
        P(),
        P("shard", "tensor"),
        P("shard", "tensor"),
        P("shard", "tensor"),
        P("tensor"),
        P("tensor"),
        P("tensor", "shard"),
        P(),
        P("shard", None),
        P(None, "shard", "tensor"),
        P(None, "shard", "tensor"),
        P(None, "tensor", "shard"),
        P("shard"),
        P("shard", "context", None),
        P("shard", "context", None),
    )
    out_specs = (
        P("shard", "context", None),
        P("shard", "context", None),
        P(),
        P("shard", "tensor"),
        P("shard", "tensor"),
        P("shard", "tensor"),
        P("tensor"),
        P("tensor"),
        P("tensor", "shard"),
        P(),
        P("shard", None),
        P(None, "shard", "tensor"),
        P(None, "shard", "tensor"),
        P(None, "tensor", "shard"),
    )

    return jax.shard_map(body, mesh=mesh, in_specs=in_specs, out_specs=out_specs, check_vma=False)
```

profile of v0, /device:TPU:0, one launch (start us, length us, event | category | flops | bytes accessed | tf_op | source)
XLA Modules:
  0.0 881.2 jit_solution(4084821147329824300)
XLA Ops:
  0.7 2.0 constant_dynamic-update-slice_fusion.2
  2.7 1.9 constant_dynamic-update-slice_fusion.1
  5.4 3.0 collective-permute-start.1
  10.2 1.8 constant_dynamic-slice_fusion.16
  12.0 2.4 copy.100
  14.4 2.7 dynamic-slice_bitcast_fusion
  17.2 3.1 pad_maximum_fusion.w_own
  20.4 23.6 %collective-permute-done.1.w2 = bf16[512,1536]{1,0:T(8,128)(2,1)} collective-permute-done((bf16[512,1536]{1,0:T(8,128)(2,1)}, bf16[512,1536]{1,0:T(8,128)(2,1)}, u32[]{:S(2)}, u32[]{:S(2)}) %collective-permute-start.1) | collective-permute-done | bytes 1572896 | tf_op jit(solution)/shard_map/ppermute | solution.py:920
  44.0 6.2 fusion.33
  50.1 2.0 collective-permute-start.10
  54.2 2.0 dynamic-slice_bitcast_fusion.5
  56.9 7.3 qkv.1
  64.2 7.2 rope.1
  71.5 1.6 copy-done
  73.9 1.5 collective-permute-start.3
  75.4 1.6 multiply_convert_fusion.g_ref.refs_1_
  78.0 3.2 pad_maximum_fusion.1
  84.7 40.7 %collective-permute-done.10.w_x = bf16[3,4,512,256]{3,2,1,0:T(8,128)(2,1)} collective-permute-done((bf16[3,4,512,256]{3,2,1,0:T(8,128)(2,1)}, bf16[3,4,512,256]{3,2,1,0:T(8,128)(2,1)}, u32[]{:S(2)}, u32[]{:S(2)}) %collective-permute-start.10) | collective-permute-done | bytes 3145760 | tf_op jit(solution)/shard_map/ppermute | solution.py:920
  128.2 11.4 %attention.1 = (bf16[512,512]{1,0:T(8,128)(2,1)S(1)}, f32[8,512]{1,0:T(8,128)S(1)}, bf16[512,2048]{1,0:T(8,128)(2,1)}) custom-call(s32[3]{0:T(128)S(1)} %add_multiply_fusion.base, bf16[512,512]{1,0:T(8,128)(2,1)S(1)} %copy-done.19, bf16[1024,1024]{1,0:T(8,128)(2,1)} %copy-done.37, bf16[1024,1024]{1,0:T(8,128)(2,1)} %copy-done.37, ...), custom_call_target="tpu_custom_call" | custom-call | flops 5368709120 | bytes 2097152 | tf_op jit(solution)/shard_map/attention/pallas_call | solution.py:797
  139.6 85.0 %shard_map.263 = (bf16[512,2048]{1,0:T(8,128)(2,1)}, f32[128,2048]{1,0:T(8,128)}, f32[128,1]{1,0:T(8,128)}) custom-call(bf16[512,2048]{1,0:T(8,128)(2,1)} %get-tuple-element.74.refs_0_, bf16[512,2048]{1,0:T(8,128)(2,1)} %copy-done.6, f32[1,2048]{1,0:T(1,128)} %bitcast.92), custom_call_target="tpu_custom_call" | custom-call | flops 12582912000 | bytes 8388608 | tf_op jit(solution)/shard_map/pallas_call | solution.py:429
  224.5 1.6 collective-permute-start.12
  229.2 3.3 slice.133.g_ref
  235.8 30.8 %collective-permute-done.12.h_ref = bf16[512,2048]{1,0:T(8,128)(2,1)} collective-permute-done((bf16[512,2048]{1,0:T(8,128)(2,1)}, bf16[512,2048]{1,0:T(8,128)(2,1)}, u32[]{:S(2)}, u32[]{:S(2)}) %collective-permute-start.12) | collective-permute-done | bytes 2097184 | tf_op jit(solution)/shard_map/ppermute | solution.py:923
  266.5 2.3 fusion.38
  271.8 32.6 %shard_map.264 = (f32[512,2048]{1,0:T(8,128)}, f32[512,2048]{1,0:T(8,128)}, f32[512,8]{1,0:T(8,128)}, bf16[4,3,4,256,512]{4,3,2,1,0:T(8,128)(2,1)}) custom-call(bf16[512,2048]{1,0:T(8,128)(2,1)} %get-tuple-element.75.h_ref.refs_2_, bf16[512,2048]{1,0:T(8,128)(2,1)} %multiply_convert_fusion.g_ref.refs_1_, f32[512,8]{1,0:T(8,128)} %dynamic-slice_select_fusion.coef_ref, ...), custom_call_target="tpu_custom_call" | custom-call | flops 19327352832 | bytes 58720256 | tf_op jit(solution)/shard_map/pallas_call | solution.py:159
  304.3 37.7 %shard_map.265 = (f32[512,2048]{1,0:T(8,128)}, f32[512,2048]{1,0:T(8,128)}, f32[512,8]{1,0:T(8,128)}, bf16[3,4,256,512]{3,2,1,0:T(8,128)(2,1)}, bf16[3,4,256,512]{3,2,1,0:T(8,128)(2,1)}) custom-call(bf16[512,2048]{1,0:T(8,128)(2,1)} %collective-permute-done.12.h_ref, bf16[512,2048]{1,0:T(8,128)(2,1)} %slice.133.g_ref, f32[512,8]{1,0:T(8,128)} %fusion.17.coef_ref, ...), custom_call_target="tpu_custom_call" | custom-call | flops 19327352832 | bytes 58720256 | tf_op jit(solution)/shard_map/pallas_call | solution.py:159
  342.0 35.6 %shard_map.266 = (f32[512,2048]{1,0:T(8,128)}, f32[512,2048]{1,0:T(8,128)}, f32[512,8]{1,0:T(8,128)}, bf16[4,3,4,256,512]{4,3,2,1,0:T(8,128)(2,1)}) custom-call(bf16[512,2048]{1,0:T(8,128)(2,1)} %collective-permute-done.12.h_ref, bf16[512,2048]{1,0:T(8,128)(2,1)} %slice.133.g_ref, f32[512,8]{1,0:T(8,128)} %fusion.17.coef_ref, ...), custom_call_target="tpu_custom_call" | custom-call | flops 19327352832 | bytes 58720256 | tf_op jit(solution)/shard_map/pallas_call | solution.py:159
  378.6 2.7 convert.18
  382.0 1.6 convert_element_type.133
  383.7 1.5 collective-permute-start.16
  385.2 1.6 fusion.14
  387.2 40.2 %shard_map.267 = (f32[512,2048]{1,0:T(8,128)}, f32[512,2048]{1,0:T(8,128)}, f32[512,8]{1,0:T(8,128)}, bf16[3,4,256,512]{3,2,1,0:T(8,128)(2,1)}, bf16[3,4,256,512]{3,2,1,0:T(8,128)(2,1)}) custom-call(bf16[512,2048]{1,0:T(8,128)(2,1)} %get-tuple-element.75.h_ref.refs_2_, bf16[512,2048]{1,0:T(8,128)(2,1)} %multiply_convert_fusion.g_ref.refs_1_, ...), custom_call_target="tpu_custom_call" | custom-call | flops 19327352832 | bytes 58720256 | tf_op jit(solution)/shard_map/pallas_call | solution.py:159
  427.5 1.6 collective-permute-start.21
  429.5 2.9 collective-permute-done.16
  432.5 4.9 add_convert_fusion.1.refs_5_
  437.4 42.2 %collective-permute-done.14 = bf16[512,2176]{1,0:T(8,128)(2,1)} collective-permute-done((bf16[512,2176]{1,0:T(8,128)(2,1)}, bf16[512,2176]{1,0:T(8,128)(2,1)}, u32[]{:S(2)}, u32[]{:S(2)}) %collective-permute-start.14) | collective-permute-done | bytes 2228256 | tf_op jit(solution)/shard_map/ppermute | solution.py:923
  481.0 2.1 convert_element_type.129
  484.0 2.1 fusion.10.refs_0_
  486.1 81.9 %shard_map.268 = (bf16[512,2048]{1,0:T(8,128)(2,1)}, f32[128,2048]{1,0:T(8,128)}, f32[1,2048]{1,0:T(1,128)}) custom-call(bf16[512,2048]{1,0:T(8,128)(2,1)} %fusion.10.refs_0_, bf16[512,2048]{1,0:T(8,128)(2,1)} %multiply_convert_fusion.g_ref.refs_1_, f32[128,2048]{1,0:T(8,128)} %get-tuple-element.88.refs_2_.refs_6_, f32[128,1]{1,0:T(8,128)} %get-tuple-element.89.refs_3_, ...), custom_call_target="tpu_custom_call" | custom-call | flops 12582912000 | bytes 8388608 | tf_op jit(solution)/shard_map/pallas_call | solution.py:429
  568.0 1.7 copy-done.21
  569.7 3.7 shard_map.271
  573.3 1.6 collective-permute-start.19
  574.9 13.8 %attention_back.1 = (f32[512,512]{1,0:T(8,128)S(1)}, f32[1024,512]{1,0:T(8,128)}, f32[1024,512]{1,0:T(8,128)}) custom-call(s32[3]{0:T(128)S(1)} %add_multiply_fusion.base, bf16[512,2048]{1,0:T(8,128)(2,1)} %get-tuple-element.90.da_ref.refs_0_, bf16[512,512]{1,0:T(8,128)(2,1)S(1)} %copy-done.20, bf16[1024,1024]{1,0:T(8,128)(2,1)} %copy-done.37, ...), custom_call_target="tpu_custom_call" | custom-call | flops 3758096384 | bytes 6291456 | tf_op jit(solution)/shard_map/attention_back/pallas_call | solution.py:860
  595.0 2.0 add_convert_fusion.5
  597.5 4.1 add_convert_fusion.own_ref
  601.6 1.6 collective-permute-start.22
  603.2 4.8 add_convert_fusion.3
  610.0 9.7 %collective-permute-done.15.far_ref = bf16[512,1024]{1,0:T(8,128)(2,1)} collective-permute-done((bf16[512,1024]{1,0:T(8,128)(2,1)}, bf16[512,1024]{1,0:T(8,128)(2,1)}, u32[]{:S(2)}, u32[]{:S(2)}) %collective-permute-start.15) | collective-permute-done | bytes 1048608 | tf_op jit(solution)/shard_map/ppermute | solution.py:923
  619.8 9.4 %qk_back.1 = (bf16[512,1536]{1,0:T(8,128)(2,1)S(1)}, f32[8,512]{1,0:T(8,128)S(1)}, f32[16,512]{1,0:T(8,128)S(1)}) custom-call(f32[512,512]{1,0:T(8,128)S(1)} %copy-done.8, f32[1024,512]{1,0:T(8,128)S(1)} %copy-done.2, f32[1024,512]{1,0:T(8,128)S(1)} %copy-done.3, bf16[512,1024]{1,0:T(8,128)(2,1)} %collective-permute-done.15.far_ref, ...), custom_call_target="tpu_custom_call" | custom-call | flops 524288000 | bytes 7864320 | tf_op jit(solution)/shard_map/qk_back/pallas_call | solution.py:607
  634.5 12.1 %shard_map.270 = (bf16[512,1664]{1,0:T(8,128)(2,1)S(1)}, bf16[512,1664]{1,0:T(8,128)(2,1)}) custom-call(bf16[512,2048]{1,0:T(8,128)(2,1)} %copy-done.22, bf16[512,1536]{1,0:T(8,128)(2,1)S(1)} %copy-done.17, bf16[512,2048]{1,0:T(8,128)(2,1)} %get-tuple-element.75.h_ref.refs_2_, bf16[512,128]{1,0:T(8,128)(2,1)S(1)} %pad.23.refs_3_), custom_call_target="tpu_custom_call" | custom-call | flops 3489660928 | bytes 4194304 | tf_op jit(solution)/shard_map/pallas_call | solution.py:737
  647.2 7.2 fusion.11.refs_0_
  654.5 156.4 %shard_map.269 = (bf16[512,2048]{1,0:T(8,128)(2,1)}, f32[1,2048]{1,0:T(1,128)}, bf16[512,2048]{1,0:T(8,128)(2,1)}) custom-call(bf16[512,2048]{1,0:T(8,128)(2,1)} %fusion.11.refs_0_, bf16[512,2048]{1,0:T(8,128)(2,1)} %copy-done.6, f32[128,2048]{1,0:T(8,128)} %get-tuple-element.97.refs_2_, f32[512,1]{1,0:T(8,128)} %copy-done.23, f32[1,2048]{1,0:T(1,128)} %bitcast.78, ...), custom_call_target="tpu_custom_call" | custom-call | flops 12582912000 | bytes 8388608 | tf_op jit(solution)/shard_map/pallas_call | solution.py:429
  811.7 3.1 add_convert_fusion.2
  816.9 26.9 %gains.1 = f32[40,128]{1,0:T(8,128)} custom-call(f32[40,128]{1,0:T(8,128)} %bitcast.81), custom_call_target="tpu_custom_call" | custom-call | flops 10000000 | bytes 100000 | tf_op jit(solution)/shard_map/gains/pallas_call | solution.py:675
  843.9 1.7 constant_dynamic-slice_fusion.15
  846.2 1.6 maximum_bitcast_fusion
  848.6 1.6 maximum_bitcast_fusion.1
  850.3 2.3 add_bitcast_fusion
  852.6 2.5 copy.98
  855.1 5.8 finish.3
  860.9 5.8 finish.4
  866.7 9.1 %finish.5 = (f32[16,512,256]{2,1,0:T(8,128)}, f32[16,512,256]{2,1,0:T(8,128)}, f32[16,256,512]{2,1,0:T(8,128)}) custom-call(s32[8]{0:T(128)S(1)} %pad_add_fusion.places, bf16[3,4,256,512]{3,2,1,0:T(8,128)(2,1)S(1)} %add_convert_fusion.own_ref, ...), custom_call_target="tpu_custom_call", output_to_operand_aliasing={{0}: (3, {}), {1}: (4, {}), {2}: (5, {})} | custom-call | bytes 18874368 | tf_op jit(solution)/shard_map/finish/pallas_call | solution.py:203
  875.8 2.3 convert_add_fusion
  878.1 1.8 fusion.34
  (210 shorter events, 46.6 us)
Async XLA Ops:
  0.6 4.0 copy-start.38
  0.7 7.8 copy-start.39
  0.7 8.0 copy-start.40
  5.4 38.5 %collective-permute-start.1 = (bf16[512,1536]{1,0:T(8,128)(2,1)}, bf16[512,1536]{1,0:T(8,128)(2,1)}, u32[]{:S(2)}, u32[]{:S(2)}) collective-permute-start(bf16[512,1536]{1,0:T(8,128)(2,1)} %constant_dynamic-update-slice_fusion.w0), channel_id=1, source_target_pairs={{0,16},{8,24},{16,0},{24,8},{1,17},{9,25},{17,1},{25,9},{2,18},{10... | collective-permute-start | bytes 4718600 | tf_op jit(solution)/shard_map/ppermute | solution.py:920
  8.4 48.2 %collective-permute-start = (bf16[512,1536]{1,0:T(8,128)(2,1)}, bf16[512,1536]{1,0:T(8,128)(2,1)}, u32[]{:S(2)}, u32[]{:S(2)}) collective-permute-start(bf16[512,1536]{1,0:T(8,128)(2,1)} %constant_dynamic-update-slice_fusion.w0), channel_id=1, source_target_pairs={{0,8},{8,0},{16,24},{24,16},{1,9},{9,1},{17,25},{25,17},{2,10},{10... | collective-permute-start | bytes 4718600 | tf_op jit(solution)/shard_map/ppermute | solution.py:917
  9.7 72.6 %collective-permute-start.4 = (bf16[512,640]{1,0:T(8,128)(2,1)}, bf16[512,640]{1,0:T(8,128)(2,1)}, u32[]{:S(2)}, u32[]{:S(2)}) collective-permute-start(bf16[512,640]{1,0:T(8,128)(2,1)} %fusion.16), channel_id=1, source_target_pairs={{0,8},{8,0},{16,24},{24,16},{1,9},{9,1},{17,25},{25,17},{2,10},{10... | collective-permute-start | bytes 1966088 | tf_op jit(solution)/shard_map/ppermute | solution.py:917
  10.2 66.9 %collective-permute-start.5 = (bf16[512,640]{1,0:T(8,128)(2,1)}, bf16[512,640]{1,0:T(8,128)(2,1)}, u32[]{:S(2)}, u32[]{:S(2)}) collective-permute-start(bf16[512,640]{1,0:T(8,128)(2,1)} %fusion.16), channel_id=1, source_target_pairs={{0,16},{8,24},{16,0},{24,8},{1,17},{9,25},{17,1},{25,9},{2,18},{10... | collective-permute-start | bytes 1966088 | tf_op jit(solution)/shard_map/ppermute | solution.py:920
  14.4 2.9 copy-start.25
  20.4 32.5 %copy-start.46 = (f32[2048]{0:T(1024)S(1)}, f32[2048]{0:T(1024)}, u32[]{:S(2)}) copy-start(f32[2048]{0:T(1024)} %param.24) | copy-start | bytes 24580
  20.4 32.5 %copy-start.47 = (f32[2048]{0:T(1024)S(1)}, f32[2048]{0:T(1024)}, u32[]{:S(2)}) copy-start(f32[2048]{0:T(1024)} %param.17) | copy-start | bytes 24580
  44.0 12.9 %collective-permute-start.2 = (bf16[512,1536]{1,0:T(8,128)(2,1)}, bf16[512,1536]{1,0:T(8,128)(2,1)}, u32[]{:S(2)}, u32[]{:S(2)}) collective-permute-start(bf16[512,1536]{1,0:T(8,128)(2,1)} %collective-permute-done.1.w2), channel_id=1, source_target_pairs={{0,8},{8,0},{16,24},{24,16},{1,9},{9,1},{17,25},{25,17},{2,10},{10... | collective-permute-start | bytes 4718600 | tf_op jit(solution)/shard_map/ppermute | solution.py:917
  50.1 4.1 copy-start.33
  50.1 75.3 %collective-permute-start.10 = (bf16[3,4,512,256]{3,2,1,0:T(8,128)(2,1)}, bf16[3,4,512,256]{3,2,1,0:T(8,128)(2,1)}, u32[]{:S(2)}, u32[]{:S(2)}) collective-permute-start(bf16[3,4,512,256]{3,2,1,0:T(8,128)(2,1)} %get-tuple-element.188), channel_id=1, source_target_pairs={{0,16},{8,24},{16,0},{24,8},{1,17},{9,25},{17,1},{25,9},{2,18},{10... | collective-permute-start | bytes 9437192 | tf_op jit(solution)/shard_map/ppermute | solution.py:920
  53.0 3.9 copy-start.15
  54.2 10.0 %copy-start.4 = (f32[512,128]{1,0:T(8,128)}, f32[512,128]{1,0:T(8,128)S(1)}, u32[]{:S(2)}) copy-start(f32[512,128]{1,0:T(8,128)S(1)} %get-tuple-element.245.sin_ref) | copy-start | bytes 786436
  56.6 7.6 copy-start.6
  56.6 215.2 %collective-permute-start.7 = (bf16[3,8,512,256]{3,2,1,0:T(8,128)(2,1)}, bf16[3,8,512,256]{3,2,1,0:T(8,128)(2,1)}, u32[]{:S(2)}, u32[]{:S(2)}) collective-permute-start(bf16[3,8,512,256]{3,2,1,0:T(8,128)(2,1)} %pad_maximum_fusion.w_own), channel_id=1, source_target_pairs={{0,8},{8,0},{16,24},{24,16},{1,9},{9,1},{17,25},{25,17},{2,10},{10... | collective-permute-start | bytes 18874376 | tf_op jit(solution)/shard_map/ppermute | solution.py:917
  56.9 7.3 copy-start.13
  56.9 7.3 copy-start.14
  64.2 7.3 copy-start.22
  64.2 9.7 %copy-start.23 = (f32[512,1]{1,0:T(8,128)}, f32[512,1]{1,0:T(8,128)S(1)}, u32[]{:S(2)}) copy-start(f32[512,1]{1,0:T(8,128)S(1)} %get-tuple-element.98.refs_3_) | copy-start | bytes 6148
  73.8 4.2 copy-start.18
  73.8 3.1 copy-start.45
  73.9 51.7 %collective-permute-start.3 = (bf16[512,1024]{1,0:T(8,128)(2,1)S(1)}, bf16[512,1024]{1,0:T(8,128)(2,1)}, u32[]{:S(2)}, u32[]{:S(2)}) collective-permute-start(bf16[512,1024]{1,0:T(8,128)(2,1)S(1)} %get-tuple-element.73), channel_id=1, source_target_pairs={{0,4},{4,0},{1,5},{5,1},{2,6},{6,2},{3,7},{7,3},{8,12},{12,8},{9,1... | collective-permute-start | bytes 3145736 | tf_op jit(solution)/shard_map/ppermute | solution.py:923
  77.0 7.0 collective-permute-start.6
  77.3 49.5 %copy-start.28 = (pred[512,16]{1,0:T(32,128)(4,1)}, pred[512,16]{1,0:T(32,128)(4,1)S(1)}, u32[]{:S(2)}) copy-start(pred[512,16]{1,0:T(32,128)(4,1)S(1)} %copy.88) | copy-start | bytes 24580
  82.3 151.2 %collective-permute-start.8 = (bf16[3,4,512,256]{3,2,1,0:T(8,128)(2,1)}, bf16[3,4,512,256]{3,2,1,0:T(8,128)(2,1)}, u32[]{:S(2)}, u32[]{:S(2)}) collective-permute-start(bf16[3,4,512,256]{3,2,1,0:T(8,128)(2,1)} %get-tuple-element.189), channel_id=1, source_target_pairs={{0,16},{8,24},{16,0},{24,8},{1,17},{9,25},{17,1},{25,9},{2,18},{10... | collective-permute-start | bytes 9437192 | tf_op jit(solution)/shard_map/ppermute | solution.py:920
  84.1 42.7 %copy-start.36 = (bf16[512,640]{1,0:T(8,128)(2,1)}, bf16[512,640]{1,0:T(8,128)(2,1)S(1)}, u32[]{:S(2)}) copy-start(bf16[512,640]{1,0:T(8,128)(2,1)S(1)} %collective-permute-done.6) | copy-start | bytes 1966084
  84.1 145.1 %collective-permute-start.13 = (bf16[512,2176]{1,0:T(8,128)(2,1)}, bf16[512,2176]{1,0:T(8,128)(2,1)}, u32[]{:S(2)}, u32[]{:S(2)}) collective-permute-start(bf16[512,2176]{1,0:T(8,128)(2,1)} %pad_maximum_fusion.1), channel_id=1, source_target_pairs={{0,4},{4,0},{1,5},{5,1},{2,6},{6,2},{3,7},{7,3},{8,12},{12,8},{9,1... | collective-permute-start | bytes 6684680 | tf_op jit(solution)/shard_map/ppermute | solution.py:923
  84.7 54.9 %copy-start.9 = (bf16[512,512]{1,0:T(8,128)(2,1)}, bf16[512,512]{1,0:T(8,128)(2,1)S(1)}, u32[]{:S(2)}) copy-start(bf16[512,512]{1,0:T(8,128)(2,1)S(1)} %slice.127.w3) | copy-start | bytes 1572868
  84.7 43.5 %copy-start.19 = (bf16[512,512]{1,0:T(8,128)(2,1)S(1)}, bf16[512,512]{1,0:T(8,128)(2,1)}, u32[]{:S(2)}) copy-start(bf16[512,512]{1,0:T(8,128)(2,1)} %copy-done.18) | copy-start | bytes 1572868
  125.4 146.3 %collective-permute-start.11 = (bf16[3,4,512,256]{3,2,1,0:T(8,128)(2,1)}, bf16[3,4,512,256]{3,2,1,0:T(8,128)(2,1)}, u32[]{:S(2)}, u32[]{:S(2)}) collective-permute-start(bf16[3,4,512,256]{3,2,1,0:T(8,128)(2,1)} %collective-permute-done.10.w_x), channel_id=1, source_target_pairs={{0,8},{8,0},{16,24},{24,16},{1,9},{9,1},{17,25},{25,17},{2,10},{10... | collective-permute-start | bytes 9437192 | tf_op jit(solution)/shard_map/ppermute | solution.py:917
  139.6 89.5 %slice-start = ((bf16[512,640]{1,0:T(8,128)(2,1)}), bf16[512,16]{1,0:T(8,128)(2,1)S(1)}, s32[]{:S(2)}) async-start(bf16[512,640]{1,0:T(8,128)(2,1)} %copy-done.36), calls=%async_computation | async-start | bytes 262144 | tf_op jit(solution)/shard_map/slice | solution.py:990
  224.5 42.0 %collective-permute-start.12 = (bf16[512,2048]{1,0:T(8,128)(2,1)}, bf16[512,2048]{1,0:T(8,128)(2,1)}, u32[]{:S(2)}, u32[]{:S(2)}) collective-permute-start(bf16[512,2048]{1,0:T(8,128)(2,1)} %get-tuple-element.75.h_ref.refs_2_), channel_id=1, source_target_pairs={{0,4},{4,0},{1,5},{5,1},{2,6},{6,2},{3,7},{7,3},{8,12},{12,8},{9,1... | collective-permute-start | bytes 6291464 | tf_op jit(solution)/shard_map/ppermute | solution.py:923
  229.2 4.4 copy-start.34
  233.5 108.5 %collective-permute-start.9 = (bf16[3,4,512,256]{3,2,1,0:T(8,128)(2,1)}, bf16[3,4,512,256]{3,2,1,0:T(8,128)(2,1)}, u32[]{:S(2)}, u32[]{:S(2)}) collective-permute-start(bf16[3,4,512,256]{3,2,1,0:T(8,128)(2,1)} %collective-permute-done.8.w_x), channel_id=1, source_target_pairs={{0,8},{8,0},{16,24},{24,16},{1,9},{9,1},{17,25},{25,17},{2,10},{10... | collective-permute-start | bytes 9437192 | tf_op jit(solution)/shard_map/ppermute | solution.py:917
  234.4 246.2 %copy-start.24 = (f32[512,16]{1,0:T(8,128)}, f32[512,16]{1,0:T(8,128)S(1)}, u32[]{:S(2)}) copy-start(f32[512,16]{1,0:T(8,128)S(1)} %copy.87) | copy-start | bytes 98308
  378.6 3.5 copy-start.26
  383.7 48.8 %collective-permute-start.16 = (bf16[512,2048]{1,0:T(8,128)(2,1)}, bf16[512,2048]{1,0:T(8,128)(2,1)}, u32[]{:S(2)}, u32[]{:S(2)}) collective-permute-start(bf16[512,2048]{1,0:T(8,128)(2,1)} %convert_element_type.133), channel_id=1, source_target_pairs={{0,4},{4,0},{1,5},{5,1},{2,6},{6,2},{3,7},{7,3},{8,12},{12,8},{9,1... | collective-permute-start | bytes 6291464 | tf_op jit(solution)/shard_map/ppermute | solution.py:923
  386.7 92.9 %collective-permute-start.14 = (bf16[512,2176]{1,0:T(8,128)(2,1)}, bf16[512,2176]{1,0:T(8,128)(2,1)}, u32[]{:S(2)}, u32[]{:S(2)}) collective-permute-start(bf16[512,2176]{1,0:T(8,128)(2,1)} %fusion.14), channel_id=1, source_target_pairs={{0,4},{4,0},{1,5},{5,1},{2,6},{6,2},{3,7},{7,3},{8,12},{12,8},{9,1... | collective-permute-start | bytes 6684680 | tf_op jit(solution)/shard_map/ppermute | solution.py:923
  427.5 170.0 %collective-permute-start.21 = (bf16[3,4,256,512]{3,2,1,0:T(8,128)(2,1)}, bf16[3,4,256,512]{3,2,1,0:T(8,128)(2,1)}, u32[]{:S(2)}, u32[]{:S(2)}) collective-permute-start(bf16[3,4,256,512]{3,2,1,0:T(8,128)(2,1)} %get-tuple-element.114), channel_id=1, source_target_pairs={{0,16},{8,24},{16,0},{24,8},{1,17},{9,25},{17,1},{25,9},{2,18},{10... | collective-permute-start | bytes 9437192 | tf_op jit(solution)/shard_map/ppermute | solution.py:920
  429.0 174.1 %collective-permute-start.23 = (bf16[3,4,256,512]{3,2,1,0:T(8,128)(2,1)}, bf16[3,4,256,512]{3,2,1,0:T(8,128)(2,1)}, u32[]{:S(2)}, u32[]{:S(2)}) collective-permute-start(bf16[3,4,256,512]{3,2,1,0:T(8,128)(2,1)} %get-tuple-element.116), channel_id=1, source_target_pairs={{0,16},{8,24},{16,0},{24,8},{1,17},{9,25},{17,1},{25,9},{2,18},{10... | collective-permute-start | bytes 9437192 | tf_op jit(solution)/shard_map/ppermute | solution.py:920
  432.5 48.1 %copy-start.41 = (f32[512,8]{1,0:T(8,128)S(1)}, f32[512,8]{1,0:T(8,128)}, u32[]{:S(2)}) copy-start(f32[512,8]{1,0:T(8,128)} %get-tuple-element.87) | copy-start | bytes 49156
  481.0 3.0 copy-start.27
  567.9 6.9 copy-start.10
  568.0 6.9 copy-start.20
  573.3 21.7 %collective-permute-start.19 = (bf16[512,512]{1,0:T(8,128)(2,1)S(1)}, bf16[512,512]{1,0:T(8,128)(2,1)}, u32[]{:S(2)}, u32[]{:S(2)}) collective-permute-start(bf16[512,512]{1,0:T(8,128)(2,1)S(1)} %get-tuple-element.112), channel_id=1, source_target_pairs={{0,16},{8,24},{16,0},{24,8},{1,17},{9,25},{17,1},{25,9},{2,18},{10... | collective-permute-start | bytes 1572872 | tf_op jit(solution)/shard_map/ppermute | solution.py:920
  589.6 5.3 copy-start.32
  589.6 5.4 copy-start.48
  593.4 26.3 %collective-permute-start.15 = (bf16[512,1024]{1,0:T(8,128)(2,1)}, bf16[512,1024]{1,0:T(8,128)(2,1)}, u32[]{:S(2)}, u32[]{:S(2)}) collective-permute-start(bf16[512,1024]{1,0:T(8,128)(2,1)} %pad_maximum_fusion.3), channel_id=1, source_target_pairs={{0,4},{4,0},{1,5},{5,1},{2,6},{6,2},{3,7},{7,3},{8,12},{12,8},{9,1... | collective-permute-start | bytes 3145736 | tf_op jit(solution)/shard_map/ppermute | solution.py:923
  597.0 253.3 %collective-permute-start.20 = (bf16[512,512]{1,0:T(8,128)(2,1)}, bf16[512,512]{1,0:T(8,128)(2,1)}, u32[]{:S(2)}, u32[]{:S(2)}) collective-permute-start(bf16[512,512]{1,0:T(8,128)(2,1)} %add_convert_fusion.5), channel_id=1, source_target_pairs={{0,4},{4,0},{1,5},{5,1},{2,6},{6,2},{3,7},{7,3},{8,12},{12,8},{9,1... | collective-permute-start | bytes 1572872 | tf_op jit(solution)/shard_map/ppermute | solution.py:923
  597.5 5.7 copy-start.30
  601.6 265.2 %collective-permute-start.22 = (bf16[3,4,256,512]{3,2,1,0:T(8,128)(2,1)S(1)}, bf16[3,4,256,512]{3,2,1,0:T(8,128)(2,1)}, u32[]{:S(2)}, u32[]{:S(2)}) collective-permute-start(bf16[3,4,256,512]{3,2,1,0:T(8,128)(2,1)S(1)} %add_convert_fusion.own_ref), channel_id=1, source_target_pairs={{0,4},{4,0},{1,5},{5,1},{2,6},{6,2},{3,7},{7,3},{8,12},{12,8},{9,1... | collective-permute-start | bytes 9437192 | tf_op jit(solution)/shard_map/ppermute | solution.py:923
  603.2 16.6 %copy-start.1 = (f32[512,1536]{1,0:T(8,128)S(1)}, f32[512,1536]{1,0:T(8,128)}, u32[]{:S(2)}) copy-start(f32[512,1536]{1,0:T(8,128)} %copy-done) | copy-start | bytes 9437188
  603.2 16.6 %copy-start.2 = (f32[1024,512]{1,0:T(8,128)S(1)}, f32[1024,512]{1,0:T(8,128)}, u32[]{:S(2)}) copy-start(f32[1024,512]{1,0:T(8,128)} %get-tuple-element.93.dk_ref) | copy-start | bytes 6291460
  603.2 16.6 %copy-start.3 = (f32[1024,512]{1,0:T(8,128)S(1)}, f32[1024,512]{1,0:T(8,128)}, u32[]{:S(2)}) copy-start(f32[1024,512]{1,0:T(8,128)} %get-tuple-element.94.dv_ref) | copy-start | bytes 6291460
  603.2 16.6 %copy-start.5 = (f32[512,128]{1,0:T(8,128)S(1)}, f32[512,128]{1,0:T(8,128)}, u32[]{:S(2)}) copy-start(f32[512,128]{1,0:T(8,128)} %copy-done.4) | copy-start | bytes 786436
  603.2 16.6 %copy-start.8 = (f32[512,512]{1,0:T(8,128)S(1)}, f32[512,512]{1,0:T(8,128)}, u32[]{:S(2)}) copy-start(f32[512,512]{1,0:T(8,128)} %copy-done.7) | copy-start | bytes 3145732
  603.2 16.6 %copy-start.12 = (f32[512,8]{1,0:T(8,128)S(1)}, f32[512,8]{1,0:T(8,128)}, u32[]{:S(2)}) copy-start(f32[512,8]{1,0:T(8,128)} %copy-done.11) | copy-start | bytes 49156
  608.0 253.0 %collective-permute-start.24 = (bf16[3,2,256,512]{3,2,1,0:T(8,128)(2,1)}, bf16[3,2,256,512]{3,2,1,0:T(8,128)(2,1)}, u32[]{:S(2)}, u32[]{:S(2)}) collective-permute-start(bf16[3,2,256,512]{3,2,1,0:T(8,128)(2,1)} %get-tuple-element.187.own_ref), channel_id=1, source_target_pairs={{0,4},{4,0},{1,5},{5,1},{2,6},{6,2},{3,7},{7,3},{8,12},{12,8},{9,1... | collective-permute-start | bytes 4718600 | tf_op jit(solution)/shard_map/ppermute | solution.py:923
  608.5 246.6 %collective-permute-start.25 = (bf16[3,2,256,512]{3,2,1,0:T(8,128)(2,1)}, bf16[3,2,256,512]{3,2,1,0:T(8,128)(2,1)}, u32[]{:S(2)}, u32[]{:S(2)}) collective-permute-start(bf16[3,2,256,512]{3,2,1,0:T(8,128)(2,1)} %get-tuple-element.186.own_ref), channel_id=1, source_target_pairs={{0,4},{4,0},{1,5},{5,1},{2,6},{6,2},{3,7},{7,3},{8,12},{12,8},{9,1... | collective-permute-start | bytes 4718600 | tf_op jit(solution)/shard_map/ppermute | solution.py:923
  646.6 165.1 %collective-permute-start.17 = (bf16[512,1664]{1,0:T(8,128)(2,1)}, bf16[512,1664]{1,0:T(8,128)(2,1)}, u32[]{:S(2)}, u32[]{:S(2)}) collective-permute-start(bf16[512,1664]{1,0:T(8,128)(2,1)} %get-tuple-element.109), channel_id=1, source_target_pairs={{0,16},{8,24},{16,0},{24,8},{1,17},{9,25},{17,1},{25,9},{2,18},{10... | collective-permute-start | bytes 5111816 | tf_op jit(solution)/shard_map/ppermute | solution.py:920
  654.5 157.2 %copy-start.43 = (f32[5120]{0:T(1024)S(1)}, f32[5120]{0:T(1024)}, u32[]{:S(2)}) copy-start(f32[5120]{0:T(1024)} %custom-call) | copy-start | bytes 61444
  814.8 61.0 %collective-permute-start.18 = (bf16[512,1664]{1,0:T(8,128)(2,1)}, bf16[512,1664]{1,0:T(8,128)(2,1)}, u32[]{:S(2)}, u32[]{:S(2)}) collective-permute-start(bf16[512,1664]{1,0:T(8,128)(2,1)} %add_convert_fusion.2), channel_id=1, source_target_pairs={{0,4},{4,0},{1,5},{5,1},{2,6},{6,2},{3,7},{7,3},{8,12},{12,8},{9,1... | collective-permute-start | bytes 5111816 | tf_op jit(solution)/shard_map/ppermute | solution.py:923
  (12 other events, 17.8 us)
where the time goes:
time: 891 us; the launch traced here: 881 us
  Pallas kernels  582 us (65%)
  waiting for transfers between devices  150 us (17%)
  local copies, waits for them, and re-layouts  55.4 us (6%)
  other arithmetic  55.3 us (6%)
  starting transfers between devices  23.7 us (3%)
  matrix products  12.3 us (1%)
    pallas_call x3, Pallas kernels, line_call(): pl.pallas_call(functools.partial(line_kernel, n, subs, kinds), in_specs=[...  323 us
    pallas_call x4, Pallas kernels, moe_call(): pl.pallas_call(functools.partial(moe_kernel, first, partial, final, base,...  146 us
    ppermute x11, waiting for transfers between devices, to_y(): return lax.ppermute(a, 'context', [(0, 1), (1, 0)])  85.6 us
    ppermute x8, waiting for transfers between devices, to_x(): return lax.ppermute(a, 'shard', [(s, s ^ 2) for s in range(shards)])  64.3 us
    pallas_call x1, Pallas kernels, gains_call(): pl.pallas_call(functools.partial(gains_kernel, sizes, both), in_specs=[vm...  26.9 us
    unnamed x116, local copies, waits for them, and re-layouts  21.4 us
    pallas_call x3, Pallas kernels, finish_call(): pl.pallas_call(functools.partial(finish_kernel, count, other is not None)...  20.7 us
  transfers between devices with their start and end apart: 26, of which 6 were waited for; matrix products, arithmetic and copies ran while one was open for 11% of the time, Pallas kernels for 62%

commit v1 on v0

--- a/solution.py
+++ b/solution.py
@@ -1,4 +1,5 @@
 import functools
+import heapq
 
 import jax
 import jax.numpy as jnp
@@ -289,126 +290,160 @@
     pl.semaphore_wait(barrier, sum(here.astype(jnp.int32) for here, _ in peers))
 
 
+def line_plan(n, subs):
+    waiting = {(z, way): [] for z in range(n) for way in (0, 1)}
+    free = dict.fromkeys(waiting, 0.0)
+    got, sent, events = {}, [[] for _ in range(n)], []
+    message, latency = 1.0, 0.2
+
+    def post(t, *what):
+        heapq.heappush(events, (t, len(seen), what))
+        seen.append(0)
+
+    def enqueue(t, z, way, kind, b, s):
+        if 0 <= z + 2 * way - 1 < n:
+            waiting[z, way].append((kind, s, -abs(b - z), b))
+            post(t, 0, z, way)
+
+    seen = []
+    for z, way in ((0, 1), (n - 1, 0)):
+        for s in range(subs):
+            for b in range(n):
+                if b != z:
+                    enqueue(0.0, z, way, 0, b, s)
+    while events:
+        t, _, (arrived, z, way, *m) = heapq.heappop(events)
+        if not arrived:
+            if waiting[z, way] and free[z, way] <= t:
+                waiting[z, way].sort()
+                kind, s, _, b = waiting[z, way].pop(0)
+                free[z, way] = t + message
+                sent[z].append((kind, way, b, s))
+                post(t + message, 0, z, way)
+                post(t + message + latency, 1, z + 2 * way - 1, way, kind, b, s)
+            continue
+        kind, b, s = m
+        if kind or b != z:
+            enqueue(t, z, way, kind, b, s)
+            continue
+        got[z, s] = got.get((z, s), 0) + 1
+        if got[z, s] == (z > 0) + (z < n - 1):
+            for w in (0, 1):
+                enqueue(t, z, w, 1, z, s)
+    plans = []
+    for z in range(n):
+        plan = []
+        for kind, way, b, s in sent[z]:
+            step = ("own", s) if kind and b == z else ("gather" if kind else "sum", way, b, s)
+            if step not in plan:
+                plan.append(step)
+        plans.append(plan)
+    return plans
+
+
 def line_kernel(n, subs, streams, *refs):
     refs = list(refs)
     ins = [[refs.pop(0) for _ in range(1 + extra)] for _, extra, _ in streams]
     outs = [[refs.pop(0) for _ in range(1 + more)] for _, _, more in streams]
-    scratch = [[refs.pop(0) for _ in range(3)] for _ in streams]
-    z = lax.axis_index("tensor")
-    inner = (z > 0, z < n - 1)
-    side = (z - 1, z + 1)
-    meet([(inner[0], z - 1), (inner[1], z + 1)])
-
-    class Stream:
-        def __init__(self, finish, part_ref, extras, out_ref, more, buf, total, sems):
-            self.finish, self.part, self.extras, self.out = finish, part_ref, extras, out_ref
-            self.more, self.buf, self.total, self.sems = more, buf, total, sems
-            self.block = part_ref.shape[0] // n
-            self.size = self.block // subs
-
-        def rows(self, b, s):
-            return pl.ds(pl.multiple_of(b * self.block + s * self.size, self.size), self.size)
-
-        def copy(self, kind, way, b, s):
-            at = self.rows(b, s)
+    bufs = [[refs.pop(0) for _ in range(2)] for _ in streams]
+    here = lax.axis_index("tensor")
+    tokens, _ = ins[0][0].shape
+    block = tokens // n
+    size = block // subs
+    piece = min(16, size)
+    for more in outs:
+        for ref in more[1:]:
+            if ref.shape[0] == 1:
+                ref[...] = jnp.zeros_like(ref)
+    meet([(here > 0, here - 1), (here < n - 1, here + 1)])
+
+    def device(z):
+        inner = (z > 0, z < n - 1)
+
+        def copy(kind, way, b, s):
+            flow, s = divmod(s, subs)
+            buf, sems = bufs[flow]
+            at = pl.ds(b * block + s * size, size)
+            edge = z == (0 if way else n - 1)
+            dst = outs[flow][0].at[at] if kind else buf.at[way, 1, at]
+            src = dst if kind else ins[flow][0].at[at] if edge else buf.at[way, 0, at]
             return pltpu.make_async_remote_copy(
-                src_ref=self.out.at[at] if kind else self.buf.at[way, 0, at],
-                dst_ref=self.out.at[at] if kind else self.buf.at[way, 1, at],
-                send_sem=self.sems.at[2 * kind, way, b, s],
-                recv_sem=self.sems.at[2 * kind + 1, way, b, s],
-                device_id={"tensor": side[way]},
+                src_ref=src,
+                dst_ref=dst,
+                send_sem=sems.at[2 * kind, way, b, s],
+                recv_sem=sems.at[2 * kind + 1, way, b, s],
+                device_id={"tensor": z + 2 * way - 1},
                 device_id_type=pl.DeviceIdType.MESH,
             )
 
-        def open(self, way):
-            @pl.when(jnp.logical_not(inner[1 - way]))
-            def _():
-                for s in range(subs):
-                    for i in range(1, n):
-                        b = n - i if way else i - 1
-                        self.buf[way, 0, self.rows(b, s)] = self.part[self.rows(b, s)]
-                        self.copy(0, way, b, s).start()
-
-        def pass_on(self, way, b, s):
-            @pl.when(inner[1 - way] & ((z < b) if way else (z > b)))
-            def _():
-                at = self.rows(b, s)
-                self.copy(0, way, b, s).wait_recv()
-                mine = self.part[at].astype(f32)
-                self.buf[way, 0, at] = (mine + self.buf[way, 1, at].astype(f32)).astype(bf16)
-                self.copy(0, way, b, s).start()
-
-        def own(self, s):
-            at = self.rows(z, s)
-            self.total[...] = self.part[at].astype(f32)
+        def came(kind, way, b, s):
+            flow, s = divmod(s, subs)
+            buf, sems = bufs[flow]
+            at = pl.ds(b * block + s * size, size)
+            dst = outs[flow][0].at[at] if kind else buf.at[way, 1, at]
+            pltpu.make_async_remote_copy(
+                src_ref=dst,
+                dst_ref=dst,
+                send_sem=sems.at[2 * kind, way, b, s],
+                recv_sem=sems.at[2 * kind + 1, way, b, s],
+                device_id={"tensor": z - 2 * way + 1},
+                device_id_type=pl.DeviceIdType.MESH,
+            ).wait_recv()
+
+        def own(s):
+            flow, local = divmod(s, subs)
             for way in (0, 1):
-
-                @pl.when(inner[1 - way])
-                def _(way=way):
-                    self.copy(0, way, z, s).wait_recv()
-                    self.total[...] += self.buf[way, 1, at].astype(f32)
-
-            local = pl.ds(s * self.size, self.size)
-            self.out[at] = self.finish(s, self.total[...], at, local, self.extras, self.more)
+                if inner[1 - way]:
+                    came(0, way, z, s)
+
+            def rows(i, _):
+                at = pl.multiple_of(z * block + local * size + i * piece, piece)
+                at = pl.ds(at, piece)
+                total = ins[flow][0][at].astype(f32)
+                for way in (0, 1):
+                    if inner[1 - way]:
+                        total = total + bufs[flow][0][way, 1, at].astype(f32)
+                nearby = pl.ds(pl.multiple_of(local * size + i * piece, piece), piece)
+                outs[flow][0][at] = streams[flow][0](total, at, nearby, ins[flow][1:], outs[flow][1:])
+
+            lax.fori_loop(0, size // piece, rows, None)
             for way in (0, 1):
-
-                @pl.when(inner[way])
-                def _(way=way):
-                    self.copy(1, way, z, s).start()
-
-        def forward(self, d, s):
-            for way in (0, 1):
-                b = z - d if way else z + d
-
-                @pl.when(inner[way] & ((b >= 0) if way else (b <= n - 1)))
-                def _(way=way, b=b):
-                    self.copy(1, way, b, s).wait_recv()
-                    self.copy(1, way, b, s).start()
-
-        def close(self, way, b, s):
-            ahead = (z < b) if way else (z > b)
-            past = (z > b) if way else (z < b)
-
-            @pl.when(past & jnp.logical_not(inner[way]))
-            def _():
-                self.copy(1, way, b, s).wait_recv()
-
-            @pl.when(ahead)
-            def _():
-                self.copy(0, way, b, s).wait_send()
-
-            @pl.when(inner[way] & jnp.logical_not(ahead))
-            def _():
-                self.copy(1, way, b, s).wait_send()
-
-    flows = [
-        Stream(finish, i[0], i[1:], o[0], o[1:], *c)
-        for (finish, _, _), i, o, c in zip(streams, ins, outs, scratch)
-    ]
-    for flow in flows:
-        for way in (0, 1):
-            flow.open(way)
-    for s in range(subs + 1):
-        for flow in flows:
-            if s < subs:
-                for i in range(1, n):
-                    flow.pass_on(1, n - i, s)
-                    flow.pass_on(0, i - 1, s)
-            if s:
-                flow.own(s - 1)
-                for d in range(1, n - 1):
-                    if s - 1 >= d:
-                        flow.forward(d, s - 1 - d)
-    for s in range(subs):
-        for flow in flows:
-            for d in range(1, n - 1):
-                if s + d >= subs:
-                    flow.forward(d, s)
-    for flow in flows:
-        for s in range(subs):
+                if inner[way]:
+                    copy(1, way, z, s).start()
+
+        def add(way, b, s):
+            flow, local = divmod(s, subs)
+            buf, part = bufs[flow][0], ins[flow][0]
+
+            def rows(i, _):
+                at = pl.ds(pl.multiple_of(b * block + local * size + i * piece, piece), piece)
+                buf[way, 0, at] = (part[at].astype(f32) + buf[way, 1, at].astype(f32)).astype(bf16)
+
+            lax.fori_loop(0, size // piece, rows, None)
+
+        for kind, *what in plans[z]:
+            if kind == "own":
+                own(*what)
+                continue
+            way, b, s = what
+            if inner[1 - way]:
+                came(kind == "gather", way, b, s)
+                if kind == "sum":
+                    add(way, b, s)
+            copy(int(kind == "gather"), way, b, s).start()
+        for s in range(subs * len(streams)):
             for b in range(n):
                 for way in (0, 1):
-                    flow.close(way, b, s)
+                    if not inner[way] and ((z > b) if way else (z < b)):
+                        came(1, way, b, s)
+                    if (z < b) if way else (z > b):
+                        copy(0, way, b, s).wait_send()
+                    elif inner[way]:
+                        copy(1, way, b, s).wait_send()
+
+    plans = line_plan(n, subs * len(streams))
+    for z in range(n):
+        pl.when(here == z)(functools.partial(device, z))
 
 
 def line_call(ident, n, streams):
@@ -423,7 +458,6 @@
         shapes += [jax.ShapeDtypeStruct(m, f32) for m in more]
         scratch += [
             pltpu.VMEM((2, 2, tokens, width), bf16),
-            pltpu.VMEM((tokens // n // subs, width), f32),
             pltpu.SemaphoreType.DMA((4, 2, n, subs)),
         ]
     return pl.pallas_call(
@@ -441,7 +475,7 @@
     )(*inputs)
 
 
-def after_attention(s, total, whole, local, refs, more):
+def after_attention(total, whole, local, refs, more):
     x_ref, gain_ref = refs
     y_ref, rate_ref = more
     y = x_ref[whole].astype(f32) + total
@@ -451,32 +485,31 @@
     return (y * rate * gain_ref[...]).astype(bf16)
 
 
-def norm_back(total, base, x, rate, gain_ref, grad_ref, s):
-    terms = jnp.sum(total * (x * rate), axis=0, keepdims=True)
-    grad_ref[...] = terms if s == 0 else grad_ref[...] + terms
+def norm_back(total, base, x, rate, gain_ref, grad_ref):
+    grad_ref[...] += jnp.sum(total * (x * rate), axis=0, keepdims=True)
     e = total * gain_ref[...]
     return base + rate * e - x * (rate * rate * rate) * jnp.mean(e * x, axis=-1, keepdims=True)
 
 
-def after_experts(s, total, whole, local, refs, more):
+def after_experts(total, whole, local, refs, more):
     g_ref, y_ref, rate_ref, gain_ref = refs
     dy_ref, grad_ref = more
     dy = norm_back(
-        total, g_ref[whole].astype(f32), y_ref[local], rate_ref[local], gain_ref, grad_ref, s
+        total, g_ref[whole].astype(f32), y_ref[local], rate_ref[local], gain_ref, grad_ref
     )
     dy_ref[local] = dy
     return dy.astype(bf16)
 
 
-def after_projections(s, total, whole, local, refs, more):
+def after_projections(total, whole, local, refs, more):
     x_ref, dy_ref, rate_ref, gain_ref = refs
     (grad_ref,) = more
     x = x_ref[whole].astype(f32)
-    dx = norm_back(total, dy_ref[local], x, rate_ref[whole], gain_ref, grad_ref, s)
+    dx = norm_back(total, dy_ref[local], x, rate_ref[whole], gain_ref, grad_ref)
     return dx.astype(bf16)
 
 
-def block_rows(s, total, whole, local, refs, more):
+def block_rows(total, whole, local, refs, more):
     y_ref, valid_ref = refs
     return (valid_ref[whole] * (y_ref[local] + total)).astype(bf16)
 
@@ -967,9 +1000,7 @@
         routes[:, :, None] == jnp.arange(experts, dtype=jnp.int32)[None, None, :], axis=1
     ).astype(f32)
     if pair:
-        g_far = to_y(
-            jnp.concatenate([g_all, jnp.pad(member, ((0, 0), (0, 128 - experts))).astype(bf16)], axis=1),
-        )
+        g_far = to_y(jnp.concatenate([g_all, jnp.pad(member, ((0, 0), (0, 128 - experts))).astype(bf16)], axis=1))
         g_far, member_far = g_far[:, :width], g_far[:, width : width + experts].astype(f32)
     proj, h1, rate1, squares = qkv_call(x_low, gain1, qkv)
     inv_freq = 10000.0 ** (-(2.0 * jnp.arange(HEAD_DIM // 2, dtype=f32)) / HEAD_DIM)
@@ -1011,7 +1042,9 @@
     grads, partials = None, {}
     for k, (n, t) in enumerate(order):
         final = not pair or n in partials
-        done = moe_call(10 + k, n * GROUP, *data[t], fetched[n], sums[t], partials.get(n), final)
+        done = moe_call(
+            10 + k, n * GROUP, *data[t], fetched[n], sums[t], partials.get(n), final
+        )
         sums[t] = done[:3]
         if not final:
             partials[n] = done[3]

time: 891 us -> 846 us (0.949)
  Pallas kernels: 582 us -> 533 us
    pallas_call x3, Pallas kernels: 323 us -> 252 us  [line_call(): pl.pallas_call(functools.partial(line_kernel, n, subs, kinds), in_specs=[...]
    pallas_call x4, Pallas kernels: 146 us -> 158 us  [moe_call(): pl.pallas_call(functools.partial(moe_kernel, first, partial, final, base,...]
    pallas_call x1, Pallas kernels: 26.9 us -> 37 us  [gains_call(): pl.pallas_call(functools.partial(gains_kernel, sizes, both), in_specs=[vm...]
  transfers between devices with their start and end apart: 26 -> 26, of which waited for: 6 -> 6; matrix products, arithmetic and copies ran while one was open for 11% -> 12% of each run, Pallas kernels for 62% -> 58%
where the time goes in v1:
time: 846 us; the launch traced here: 836 us
  Pallas kernels  533 us (63%)
  waiting for transfers between devices  154 us (18%)
  local copies, waits for them, and re-layouts  55.4 us (7%)
  other arithmetic  55.3 us (7%)
  starting transfers between devices  23.9 us (3%)
  matrix products  12.3 us (1%)
    pallas_call x3, Pallas kernels, line_call(): pl.pallas_call(functools.partial(line_kernel, n, subs, kinds), in_specs=[...  252 us
    pallas_call x4, Pallas kernels, moe_call(): pl.pallas_call(functools.partial(moe_kernel, first, partial, final, base,...  158 us
    ppermute x11, waiting for transfers between devices, to_y(): return lax.ppermute(a, 'context', [(0, 1), (1, 0)])  90 us
    ppermute x8, waiting for transfers between devices, to_x(): return lax.ppermute(a, 'shard', [(s, s ^ 2) for s in range(shards)])  64.3 us
    pallas_call x1, Pallas kernels, gains_call(): pl.pallas_call(functools.partial(gains_kernel, sizes, both), in_specs=[vm...  37 us
    unnamed x116, local copies, waits for them, and re-layouts  21.4 us
    pallas_call x3, Pallas kernels, finish_call(): pl.pallas_call(functools.partial(finish_kernel, count, other is not None)...  20.7 us
  transfers between devices with their start and end apart: 26, of which 6 were waited for; matrix products, arithmetic and copies ran while one was open for 12% of the time, Pallas kernels for 58%

profile of v1, /device:TPU:0, one launch (start us, length us, event | category | flops | bytes accessed | tf_op | source)
XLA Modules:
  0.0 836.3 jit_solution(15691955554870365642)
XLA Ops:
  0.7 2.0 constant_dynamic-update-slice_fusion.2
  2.7 1.9 constant_dynamic-update-slice_fusion.1
  5.4 3.0 collective-permute-start.1
  10.2 1.8 constant_dynamic-slice_fusion.16
  12.0 2.4 copy.100
  14.4 2.7 dynamic-slice_bitcast_fusion
  17.2 3.1 pad_maximum_fusion.w_own
  20.4 23.6 %collective-permute-done.1.w2 = bf16[512,1536]{1,0:T(8,128)(2,1)} collective-permute-done((bf16[512,1536]{1,0:T(8,128)(2,1)}, bf16[512,1536]{1,0:T(8,128)(2,1)}, u32[]{:S(2)}, u32[]{:S(2)}) %collective-permute-start.1) | collective-permute-done | bytes 1572896 | tf_op jit(solution)/shard_map/ppermute | solution.py:953
  44.0 6.2 fusion.33
  50.1 2.0 collective-permute-start.10
  54.2 2.0 dynamic-slice_bitcast_fusion.5
  56.9 7.3 qkv.1
  64.2 7.2 rope.1
  71.5 1.6 copy-done
  75.4 1.6 multiply_convert_fusion.g_ref.refs_1_
  78.0 3.2 pad_maximum_fusion.1
  84.7 40.7 %collective-permute-done.10.w_x = bf16[3,4,512,256]{3,2,1,0:T(8,128)(2,1)} collective-permute-done((bf16[3,4,512,256]{3,2,1,0:T(8,128)(2,1)}, bf16[3,4,512,256]{3,2,1,0:T(8,128)(2,1)}, u32[]{:S(2)}, u32[]{:S(2)}) %collective-permute-start.10) | collective-permute-done | bytes 3145760 | tf_op jit(solution)/shard_map/ppermute | solution.py:953
  128.2 11.4 %attention.1 = (bf16[512,512]{1,0:T(8,128)(2,1)S(1)}, f32[8,512]{1,0:T(8,128)S(1)}, bf16[512,2048]{1,0:T(8,128)(2,1)}) custom-call(s32[3]{0:T(128)S(1)} %add_multiply_fusion.base, bf16[512,512]{1,0:T(8,128)(2,1)S(1)} %copy-done.19, bf16[1024,1024]{1,0:T(8,128)(2,1)} %copy-done.37, bf16[1024,1024]{1,0:T(8,128)(2,1)} %copy-done.37, ...), custom_call_target="tpu_custom_call" | custom-call | flops 5368709120 | bytes 2097152 | tf_op jit(solution)/shard_map/attention/pallas_call | solution.py:830
  139.6 71.6 %shard_map.263 = (bf16[512,2048]{1,0:T(8,128)(2,1)}, f32[128,2048]{1,0:T(8,128)}, f32[128,1]{1,0:T(8,128)}) custom-call(bf16[512,2048]{1,0:T(8,128)(2,1)} %get-tuple-element.74.refs_0_, bf16[512,2048]{1,0:T(8,128)(2,1)} %copy-done.6, f32[1,2048]{1,0:T(1,128)} %bitcast.92), custom_call_target="tpu_custom_call" | custom-call | flops 12582912000 | bytes 8388608 | tf_op jit(solution)/shard_map/pallas_call | solution.py:463
  211.1 1.6 collective-permute-start.12
  215.9 3.3 slice.133.g_ref
  222.4 34.9 %collective-permute-done.12.h_ref = bf16[512,2048]{1,0:T(8,128)(2,1)} collective-permute-done((bf16[512,2048]{1,0:T(8,128)(2,1)}, bf16[512,2048]{1,0:T(8,128)(2,1)}, u32[]{:S(2)}, u32[]{:S(2)}) %collective-permute-start.12) | collective-permute-done | bytes 2097184 | tf_op jit(solution)/shard_map/ppermute | solution.py:956
  257.4 2.3 fusion.38
  262.6 32.6 %shard_map.264 = (f32[512,2048]{1,0:T(8,128)}, f32[512,2048]{1,0:T(8,128)}, f32[512,8]{1,0:T(8,128)}, bf16[4,3,4,256,512]{4,3,2,1,0:T(8,128)(2,1)}) custom-call(bf16[512,2048]{1,0:T(8,128)(2,1)} %get-tuple-element.75.h_ref.refs_2_, bf16[512,2048]{1,0:T(8,128)(2,1)} %multiply_convert_fusion.g_ref.refs_1_, f32[512,8]{1,0:T(8,128)} %dynamic-slice_select_fusion.coef_ref, ...), custom_call_target="tpu_custom_call" | custom-call | flops 19327352832 | bytes 58720256 | tf_op jit(solution)/shard_map/pallas_call | solution.py:160
  295.2 37.7 %shard_map.265 = (f32[512,2048]{1,0:T(8,128)}, f32[512,2048]{1,0:T(8,128)}, f32[512,8]{1,0:T(8,128)}, bf16[3,4,256,512]{3,2,1,0:T(8,128)(2,1)}, bf16[3,4,256,512]{3,2,1,0:T(8,128)(2,1)}) custom-call(bf16[512,2048]{1,0:T(8,128)(2,1)} %collective-permute-done.12.h_ref, bf16[512,2048]{1,0:T(8,128)(2,1)} %slice.133.g_ref, f32[512,8]{1,0:T(8,128)} %fusion.17.coef_ref, ...), custom_call_target="tpu_custom_call" | custom-call | flops 19327352832 | bytes 58720256 | tf_op jit(solution)/shard_map/pallas_call | solution.py:160
  332.9 47.9 %shard_map.266 = (f32[512,2048]{1,0:T(8,128)}, f32[512,2048]{1,0:T(8,128)}, f32[512,8]{1,0:T(8,128)}, bf16[4,3,4,256,512]{4,3,2,1,0:T(8,128)(2,1)}) custom-call(bf16[512,2048]{1,0:T(8,128)(2,1)} %collective-permute-done.12.h_ref, bf16[512,2048]{1,0:T(8,128)(2,1)} %slice.133.g_ref, f32[512,8]{1,0:T(8,128)} %fusion.17.coef_ref, ...), custom_call_target="tpu_custom_call" | custom-call | flops 19327352832 | bytes 58720256 | tf_op jit(solution)/shard_map/pallas_call | solution.py:160
  381.7 2.7 convert.18
  385.1 1.6 convert_element_type.133
  386.8 1.5 collective-permute-start.16
  388.3 1.6 fusion.14
  390.4 40.0 %shard_map.267 = (f32[512,2048]{1,0:T(8,128)}, f32[512,2048]{1,0:T(8,128)}, f32[512,8]{1,0:T(8,128)}, bf16[3,4,256,512]{3,2,1,0:T(8,128)(2,1)}, bf16[3,4,256,512]{3,2,1,0:T(8,128)(2,1)}) custom-call(bf16[512,2048]{1,0:T(8,128)(2,1)} %get-tuple-element.75.h_ref.refs_2_, bf16[512,2048]{1,0:T(8,128)(2,1)} %multiply_convert_fusion.g_ref.refs_1_, ...), custom_call_target="tpu_custom_call" | custom-call | flops 19327352832 | bytes 58720256 | tf_op jit(solution)/shard_map/pallas_call | solution.py:160
  430.4 1.6 collective-permute-start.21
  432.5 3.1 collective-permute-done.16
  435.6 4.9 add_convert_fusion.1.refs_5_
  440.5 42.2 %collective-permute-done.14 = bf16[512,2176]{1,0:T(8,128)(2,1)} collective-permute-done((bf16[512,2176]{1,0:T(8,128)(2,1)}, bf16[512,2176]{1,0:T(8,128)(2,1)}, u32[]{:S(2)}, u32[]{:S(2)}) %collective-permute-start.14) | collective-permute-done | bytes 2228256 | tf_op jit(solution)/shard_map/ppermute | solution.py:956
  484.2 2.1 convert_element_type.129
  487.1 2.1 fusion.10.refs_0_
  489.2 64.9 %shard_map.268 = (bf16[512,2048]{1,0:T(8,128)(2,1)}, f32[128,2048]{1,0:T(8,128)}, f32[1,2048]{1,0:T(1,128)}) custom-call(bf16[512,2048]{1,0:T(8,128)(2,1)} %fusion.10.refs_0_, bf16[512,2048]{1,0:T(8,128)(2,1)} %multiply_convert_fusion.g_ref.refs_1_, f32[128,2048]{1,0:T(8,128)} %get-tuple-element.88.refs_2_.refs_6_, f32[128,1]{1,0:T(8,128)} %get-tuple-element.89.refs_3_, ...), custom_call_target="tpu_custom_call" | custom-call | flops 12582912000 | bytes 8388608 | tf_op jit(solution)/shard_map/pallas_call | solution.py:463
  554.1 1.7 copy-done.21
  555.8 3.6 shard_map.271
  559.4 1.6 collective-permute-start.19
  561.0 14.0 %attention_back.1 = (f32[512,512]{1,0:T(8,128)S(1)}, f32[1024,512]{1,0:T(8,128)}, f32[1024,512]{1,0:T(8,128)}) custom-call(s32[3]{0:T(128)S(1)} %add_multiply_fusion.base, bf16[512,2048]{1,0:T(8,128)(2,1)} %get-tuple-element.90.da_ref.refs_0_, bf16[512,512]{1,0:T(8,128)(2,1)S(1)} %copy-done.20, bf16[1024,1024]{1,0:T(8,128)(2,1)} %copy-done.37, ...), custom_call_target="tpu_custom_call" | custom-call | flops 3758096384 | bytes 6291456 | tf_op jit(solution)/shard_map/attention_back/pallas_call | solution.py:893
  581.4 2.0 add_convert_fusion.5
  583.8 4.1 add_convert_fusion.own_ref
  587.9 1.6 collective-permute-start.22
  589.5 4.8 add_convert_fusion.3
  596.3 9.7 %collective-permute-done.15.far_ref = bf16[512,1024]{1,0:T(8,128)(2,1)} collective-permute-done((bf16[512,1024]{1,0:T(8,128)(2,1)}, bf16[512,1024]{1,0:T(8,128)(2,1)}, u32[]{:S(2)}, u32[]{:S(2)}) %collective-permute-start.15) | collective-permute-done | bytes 1048608 | tf_op jit(solution)/shard_map/ppermute | solution.py:956
  606.1 9.4 %qk_back.1 = (bf16[512,1536]{1,0:T(8,128)(2,1)S(1)}, f32[8,512]{1,0:T(8,128)S(1)}, f32[16,512]{1,0:T(8,128)S(1)}) custom-call(f32[512,512]{1,0:T(8,128)S(1)} %copy-done.8, f32[1024,512]{1,0:T(8,128)S(1)} %copy-done.2, f32[1024,512]{1,0:T(8,128)S(1)} %copy-done.3, bf16[512,1024]{1,0:T(8,128)(2,1)} %collective-permute-done.15.far_ref, ...), custom_call_target="tpu_custom_call" | custom-call | flops 524288000 | bytes 7864320 | tf_op jit(solution)/shard_map/qk_back/pallas_call | solution.py:640
  620.8 12.1 %shard_map.270 = (bf16[512,1664]{1,0:T(8,128)(2,1)S(1)}, bf16[512,1664]{1,0:T(8,128)(2,1)}) custom-call(bf16[512,2048]{1,0:T(8,128)(2,1)} %copy-done.22, bf16[512,1536]{1,0:T(8,128)(2,1)S(1)} %copy-done.17, bf16[512,2048]{1,0:T(8,128)(2,1)} %get-tuple-element.75.h_ref.refs_2_, bf16[512,128]{1,0:T(8,128)(2,1)S(1)} %pad.23.refs_3_), custom_call_target="tpu_custom_call" | custom-call | flops 3489660928 | bytes 4194304 | tf_op jit(solution)/shard_map/pallas_call | solution.py:770
  633.5 7.2 fusion.11.refs_0_
  640.8 115.4 %shard_map.269 = (bf16[512,2048]{1,0:T(8,128)(2,1)}, f32[1,2048]{1,0:T(1,128)}, bf16[512,2048]{1,0:T(8,128)(2,1)}) custom-call(bf16[512,2048]{1,0:T(8,128)(2,1)} %fusion.11.refs_0_, bf16[512,2048]{1,0:T(8,128)(2,1)} %copy-done.6, f32[128,2048]{1,0:T(8,128)} %get-tuple-element.97.refs_2_, f32[512,1]{1,0:T(8,128)} %copy-done.23, f32[1,2048]{1,0:T(1,128)} %bitcast.78, ...), custom_call_target="tpu_custom_call" | custom-call | flops 12582912000 | bytes 8388608 | tf_op jit(solution)/shard_map/pallas_call | solution.py:463
  757.0 3.1 add_convert_fusion.2
  760.1 1.6 collective-permute-start.18
  762.3 37.0 %gains.1 = f32[40,128]{1,0:T(8,128)} custom-call(f32[40,128]{1,0:T(8,128)} %bitcast.81), custom_call_target="tpu_custom_call" | custom-call | flops 10000000 | bytes 100000 | tf_op jit(solution)/shard_map/gains/pallas_call | solution.py:708
  799.3 1.7 constant_dynamic-slice_fusion.15
  801.6 1.6 maximum_bitcast_fusion
  804.1 1.6 maximum_bitcast_fusion.1
  805.7 2.3 add_bitcast_fusion
  808.0 2.5 copy.98
  810.6 5.8 finish.3
  816.4 5.8 finish.4
  822.2 9.1 %finish.5 = (f32[16,512,256]{2,1,0:T(8,128)}, f32[16,512,256]{2,1,0:T(8,128)}, f32[16,256,512]{2,1,0:T(8,128)}) custom-call(s32[8]{0:T(128)S(1)} %pad_add_fusion.places, bf16[3,4,256,512]{3,2,1,0:T(8,128)(2,1)S(1)} %add_convert_fusion.own_ref, ...), custom_call_target="tpu_custom_call", output_to_operand_aliasing={{0}: (3, {}), {1}: (4, {}), {2}: (5, {})} | custom-call | bytes 18874368 | tf_op jit(solution)/shard_map/finish/pallas_call | solution.py:204
  831.3 2.3 convert_add_fusion
  833.6 1.8 fusion.34
  (210 shorter events, 46.6 us)
Async XLA Ops:
  0.6 4.0 copy-start.38
  0.7 7.8 copy-start.39
  0.7 8.0 copy-start.40
  5.4 38.5 %collective-permute-start.1 = (bf16[512,1536]{1,0:T(8,128)(2,1)}, bf16[512,1536]{1,0:T(8,128)(2,1)}, u32[]{:S(2)}, u32[]{:S(2)}) collective-permute-start(bf16[512,1536]{1,0:T(8,128)(2,1)} %constant_dynamic-update-slice_fusion.w0), channel_id=1, source_target_pairs={{0,16},{8,24},{16,0},{24,8},{1,17},{9,25},{17,1},{25,9},{2,18},{10... | collective-permute-start | bytes 4718600 | tf_op jit(solution)/shard_map/ppermute | solution.py:953
  8.4 48.2 %collective-permute-start = (bf16[512,1536]{1,0:T(8,128)(2,1)}, bf16[512,1536]{1,0:T(8,128)(2,1)}, u32[]{:S(2)}, u32[]{:S(2)}) collective-permute-start(bf16[512,1536]{1,0:T(8,128)(2,1)} %constant_dynamic-update-slice_fusion.w0), channel_id=1, source_target_pairs={{0,8},{8,0},{16,24},{24,16},{1,9},{9,1},{17,25},{25,17},{2,10},{10... | collective-permute-start | bytes 4718600 | tf_op jit(solution)/shard_map/ppermute | solution.py:950
  9.7 72.6 %collective-permute-start.4 = (bf16[512,640]{1,0:T(8,128)(2,1)}, bf16[512,640]{1,0:T(8,128)(2,1)}, u32[]{:S(2)}, u32[]{:S(2)}) collective-permute-start(bf16[512,640]{1,0:T(8,128)(2,1)} %fusion.16), channel_id=1, source_target_pairs={{0,8},{8,0},{16,24},{24,16},{1,9},{9,1},{17,25},{25,17},{2,10},{10... | collective-permute-start | bytes 1966088 | tf_op jit(solution)/shard_map/ppermute | solution.py:950
  10.2 66.9 %collective-permute-start.5 = (bf16[512,640]{1,0:T(8,128)(2,1)}, bf16[512,640]{1,0:T(8,128)(2,1)}, u32[]{:S(2)}, u32[]{:S(2)}) collective-permute-start(bf16[512,640]{1,0:T(8,128)(2,1)} %fusion.16), channel_id=1, source_target_pairs={{0,16},{8,24},{16,0},{24,8},{1,17},{9,25},{17,1},{25,9},{2,18},{10... | collective-permute-start | bytes 1966088 | tf_op jit(solution)/shard_map/ppermute | solution.py:953
  14.4 2.9 copy-start.25
  20.4 32.5 %copy-start.46 = (f32[2048]{0:T(1024)S(1)}, f32[2048]{0:T(1024)}, u32[]{:S(2)}) copy-start(f32[2048]{0:T(1024)} %param.24) | copy-start | bytes 24580
  20.4 32.5 %copy-start.47 = (f32[2048]{0:T(1024)S(1)}, f32[2048]{0:T(1024)}, u32[]{:S(2)}) copy-start(f32[2048]{0:T(1024)} %param.17) | copy-start | bytes 24580
  44.0 12.9 %collective-permute-start.2 = (bf16[512,1536]{1,0:T(8,128)(2,1)}, bf16[512,1536]{1,0:T(8,128)(2,1)}, u32[]{:S(2)}, u32[]{:S(2)}) collective-permute-start(bf16[512,1536]{1,0:T(8,128)(2,1)} %collective-permute-done.1.w2), channel_id=1, source_target_pairs={{0,8},{8,0},{16,24},{24,16},{1,9},{9,1},{17,25},{25,17},{2,10},{10... | collective-permute-start | bytes 4718600 | tf_op jit(solution)/shard_map/ppermute | solution.py:950
  50.1 4.1 copy-start.33
  50.1 75.3 %collective-permute-start.10 = (bf16[3,4,512,256]{3,2,1,0:T(8,128)(2,1)}, bf16[3,4,512,256]{3,2,1,0:T(8,128)(2,1)}, u32[]{:S(2)}, u32[]{:S(2)}) collective-permute-start(bf16[3,4,512,256]{3,2,1,0:T(8,128)(2,1)} %get-tuple-element.188), channel_id=1, source_target_pairs={{0,16},{8,24},{16,0},{24,8},{1,17},{9,25},{17,1},{25,9},{2,18},{10... | collective-permute-start | bytes 9437192 | tf_op jit(solution)/shard_map/ppermute | solution.py:953
  53.0 3.9 copy-start.15
  54.2 10.0 %copy-start.4 = (f32[512,128]{1,0:T(8,128)}, f32[512,128]{1,0:T(8,128)S(1)}, u32[]{:S(2)}) copy-start(f32[512,128]{1,0:T(8,128)S(1)} %get-tuple-element.245.sin_ref) | copy-start | bytes 786436
  56.6 7.6 copy-start.6
  56.6 206.0 %collective-permute-start.7 = (bf16[3,8,512,256]{3,2,1,0:T(8,128)(2,1)}, bf16[3,8,512,256]{3,2,1,0:T(8,128)(2,1)}, u32[]{:S(2)}, u32[]{:S(2)}) collective-permute-start(bf16[3,8,512,256]{3,2,1,0:T(8,128)(2,1)} %pad_maximum_fusion.w_own), channel_id=1, source_target_pairs={{0,8},{8,0},{16,24},{24,16},{1,9},{9,1},{17,25},{25,17},{2,10},{10... | collective-permute-start | bytes 18874376 | tf_op jit(solution)/shard_map/ppermute | solution.py:950
  56.9 7.3 copy-start.13
  56.9 7.3 copy-start.14
  64.2 7.3 copy-start.22
  64.2 9.7 %copy-start.23 = (f32[512,1]{1,0:T(8,128)}, f32[512,1]{1,0:T(8,128)S(1)}, u32[]{:S(2)}) copy-start(f32[512,1]{1,0:T(8,128)S(1)} %get-tuple-element.98.refs_3_) | copy-start | bytes 6148
  73.8 4.2 copy-start.18
  73.8 3.1 copy-start.45
  73.9 51.7 %collective-permute-start.3 = (bf16[512,1024]{1,0:T(8,128)(2,1)S(1)}, bf16[512,1024]{1,0:T(8,128)(2,1)}, u32[]{:S(2)}, u32[]{:S(2)}) collective-permute-start(bf16[512,1024]{1,0:T(8,128)(2,1)S(1)} %get-tuple-element.73), channel_id=1, source_target_pairs={{0,4},{4,0},{1,5},{5,1},{2,6},{6,2},{3,7},{7,3},{8,12},{12,8},{9,1... | collective-permute-start | bytes 3145736 | tf_op jit(solution)/shard_map/ppermute | solution.py:956
  77.0 7.0 collective-permute-start.6
  77.3 49.5 %copy-start.28 = (pred[512,16]{1,0:T(32,128)(4,1)}, pred[512,16]{1,0:T(32,128)(4,1)S(1)}, u32[]{:S(2)}) copy-start(pred[512,16]{1,0:T(32,128)(4,1)S(1)} %copy.88) | copy-start | bytes 24580
  82.3 137.8 %collective-permute-start.8 = (bf16[3,4,512,256]{3,2,1,0:T(8,128)(2,1)}, bf16[3,4,512,256]{3,2,1,0:T(8,128)(2,1)}, u32[]{:S(2)}, u32[]{:S(2)}) collective-permute-start(bf16[3,4,512,256]{3,2,1,0:T(8,128)(2,1)} %get-tuple-element.189), channel_id=1, source_target_pairs={{0,16},{8,24},{16,0},{24,8},{1,17},{9,25},{17,1},{25,9},{2,18},{10... | collective-permute-start | bytes 9437192 | tf_op jit(solution)/shard_map/ppermute | solution.py:953
  84.1 42.7 %copy-start.36 = (bf16[512,640]{1,0:T(8,128)(2,1)}, bf16[512,640]{1,0:T(8,128)(2,1)S(1)}, u32[]{:S(2)}) copy-start(bf16[512,640]{1,0:T(8,128)(2,1)S(1)} %collective-permute-done.6) | copy-start | bytes 1966084
  84.1 131.8 %collective-permute-start.13 = (bf16[512,2176]{1,0:T(8,128)(2,1)}, bf16[512,2176]{1,0:T(8,128)(2,1)}, u32[]{:S(2)}, u32[]{:S(2)}) collective-permute-start(bf16[512,2176]{1,0:T(8,128)(2,1)} %pad_maximum_fusion.1), channel_id=1, source_target_pairs={{0,4},{4,0},{1,5},{5,1},{2,6},{6,2},{3,7},{7,3},{8,12},{12,8},{9,1... | collective-permute-start | bytes 6684680 | tf_op jit(solution)/shard_map/ppermute | solution.py:956
  84.7 54.9 %copy-start.9 = (bf16[512,512]{1,0:T(8,128)(2,1)}, bf16[512,512]{1,0:T(8,128)(2,1)S(1)}, u32[]{:S(2)}) copy-start(bf16[512,512]{1,0:T(8,128)(2,1)S(1)} %slice.127.w3) | copy-start | bytes 1572868
  84.7 43.5 %copy-start.19 = (bf16[512,512]{1,0:T(8,128)(2,1)S(1)}, bf16[512,512]{1,0:T(8,128)(2,1)}, u32[]{:S(2)}) copy-start(bf16[512,512]{1,0:T(8,128)(2,1)} %copy-done.18) | copy-start | bytes 1572868
  125.4 137.2 %collective-permute-start.11 = (bf16[3,4,512,256]{3,2,1,0:T(8,128)(2,1)}, bf16[3,4,512,256]{3,2,1,0:T(8,128)(2,1)}, u32[]{:S(2)}, u32[]{:S(2)}) collective-permute-start(bf16[3,4,512,256]{3,2,1,0:T(8,128)(2,1)} %collective-permute-done.10.w_x), channel_id=1, source_target_pairs={{0,8},{8,0},{16,24},{24,16},{1,9},{9,1},{17,25},{25,17},{2,10},{10... | collective-permute-start | bytes 9437192 | tf_op jit(solution)/shard_map/ppermute | solution.py:950
  139.6 76.2 %slice-start = ((bf16[512,640]{1,0:T(8,128)(2,1)}), bf16[512,16]{1,0:T(8,128)(2,1)S(1)}, s32[]{:S(2)}) async-start(bf16[512,640]{1,0:T(8,128)(2,1)} %copy-done.36), calls=%async_computation | async-start | bytes 262144 | tf_op jit(solution)/shard_map/slice | solution.py:1021
  211.1 46.2 %collective-permute-start.12 = (bf16[512,2048]{1,0:T(8,128)(2,1)}, bf16[512,2048]{1,0:T(8,128)(2,1)}, u32[]{:S(2)}, u32[]{:S(2)}) collective-permute-start(bf16[512,2048]{1,0:T(8,128)(2,1)} %get-tuple-element.75.h_ref.refs_2_), channel_id=1, source_target_pairs={{0,4},{4,0},{1,5},{5,1},{2,6},{6,2},{3,7},{7,3},{8,12},{12,8},{9,1... | collective-permute-start | bytes 6291464 | tf_op jit(solution)/shard_map/ppermute | solution.py:956
  215.9 4.4 copy-start.34
  220.2 112.7 %collective-permute-start.9 = (bf16[3,4,512,256]{3,2,1,0:T(8,128)(2,1)}, bf16[3,4,512,256]{3,2,1,0:T(8,128)(2,1)}, u32[]{:S(2)}, u32[]{:S(2)}) collective-permute-start(bf16[3,4,512,256]{3,2,1,0:T(8,128)(2,1)} %collective-permute-done.8.w_x), channel_id=1, source_target_pairs={{0,8},{8,0},{16,24},{24,16},{1,9},{9,1},{17,25},{25,17},{2,10},{10... | collective-permute-start | bytes 9437192 | tf_op jit(solution)/shard_map/ppermute | solution.py:950
  221.1 262.6 %copy-start.24 = (f32[512,16]{1,0:T(8,128)}, f32[512,16]{1,0:T(8,128)S(1)}, u32[]{:S(2)}) copy-start(f32[512,16]{1,0:T(8,128)S(1)} %copy.87) | copy-start | bytes 98308
  381.7 3.5 copy-start.26
  386.8 48.8 %collective-permute-start.16 = (bf16[512,2048]{1,0:T(8,128)(2,1)}, bf16[512,2048]{1,0:T(8,128)(2,1)}, u32[]{:S(2)}, u32[]{:S(2)}) collective-permute-start(bf16[512,2048]{1,0:T(8,128)(2,1)} %convert_element_type.133), channel_id=1, source_target_pairs={{0,4},{4,0},{1,5},{5,1},{2,6},{6,2},{3,7},{7,3},{8,12},{12,8},{9,1... | collective-permute-start | bytes 6291464 | tf_op jit(solution)/shard_map/ppermute | solution.py:956
  389.9 92.9 %collective-permute-start.14 = (bf16[512,2176]{1,0:T(8,128)(2,1)}, bf16[512,2176]{1,0:T(8,128)(2,1)}, u32[]{:S(2)}, u32[]{:S(2)}) collective-permute-start(bf16[512,2176]{1,0:T(8,128)(2,1)} %fusion.14), channel_id=1, source_target_pairs={{0,4},{4,0},{1,5},{5,1},{2,6},{6,2},{3,7},{7,3},{8,12},{12,8},{9,1... | collective-permute-start | bytes 6684680 | tf_op jit(solution)/shard_map/ppermute | solution.py:956
  430.4 153.4 %collective-permute-start.21 = (bf16[3,4,256,512]{3,2,1,0:T(8,128)(2,1)}, bf16[3,4,256,512]{3,2,1,0:T(8,128)(2,1)}, u32[]{:S(2)}, u32[]{:S(2)}) collective-permute-start(bf16[3,4,256,512]{3,2,1,0:T(8,128)(2,1)} %get-tuple-element.114), channel_id=1, source_target_pairs={{0,16},{8,24},{16,0},{24,8},{1,17},{9,25},{17,1},{25,9},{2,18},{10... | collective-permute-start | bytes 9437192 | tf_op jit(solution)/shard_map/ppermute | solution.py:953
  432.0 157.5 %collective-permute-start.23 = (bf16[3,4,256,512]{3,2,1,0:T(8,128)(2,1)}, bf16[3,4,256,512]{3,2,1,0:T(8,128)(2,1)}, u32[]{:S(2)}, u32[]{:S(2)}) collective-permute-start(bf16[3,4,256,512]{3,2,1,0:T(8,128)(2,1)} %get-tuple-element.116), channel_id=1, source_target_pairs={{0,16},{8,24},{16,0},{24,8},{1,17},{9,25},{17,1},{25,9},{2,18},{10... | collective-permute-start | bytes 9437192 | tf_op jit(solution)/shard_map/ppermute | solution.py:953
  435.6 48.1 %copy-start.41 = (f32[512,8]{1,0:T(8,128)S(1)}, f32[512,8]{1,0:T(8,128)}, u32[]{:S(2)}) copy-start(f32[512,8]{1,0:T(8,128)} %get-tuple-element.87) | copy-start | bytes 49156
  484.1 3.0 copy-start.27
  554.1 6.9 copy-start.10
  554.1 6.9 copy-start.20
  559.4 21.9 %collective-permute-start.19 = (bf16[512,512]{1,0:T(8,128)(2,1)S(1)}, bf16[512,512]{1,0:T(8,128)(2,1)}, u32[]{:S(2)}, u32[]{:S(2)}) collective-permute-start(bf16[512,512]{1,0:T(8,128)(2,1)S(1)} %get-tuple-element.112), channel_id=1, source_target_pairs={{0,16},{8,24},{16,0},{24,8},{1,17},{9,25},{17,1},{25,9},{2,18},{10... | collective-permute-start | bytes 1572872 | tf_op jit(solution)/shard_map/ppermute | solution.py:953
  575.9 5.3 copy-start.32
  575.9 5.4 copy-start.48
  579.7 26.3 %collective-permute-start.15 = (bf16[512,1024]{1,0:T(8,128)(2,1)}, bf16[512,1024]{1,0:T(8,128)(2,1)}, u32[]{:S(2)}, u32[]{:S(2)}) collective-permute-start(bf16[512,1024]{1,0:T(8,128)(2,1)} %pad_maximum_fusion.3), channel_id=1, source_target_pairs={{0,4},{4,0},{1,5},{5,1},{2,6},{6,2},{3,7},{7,3},{8,12},{12,8},{9,1... | collective-permute-start | bytes 3145736 | tf_op jit(solution)/shard_map/ppermute | solution.py:956
  583.3 222.4 %collective-permute-start.20 = (bf16[512,512]{1,0:T(8,128)(2,1)}, bf16[512,512]{1,0:T(8,128)(2,1)}, u32[]{:S(2)}, u32[]{:S(2)}) collective-permute-start(bf16[512,512]{1,0:T(8,128)(2,1)} %add_convert_fusion.5), channel_id=1, source_target_pairs={{0,4},{4,0},{1,5},{5,1},{2,6},{6,2},{3,7},{7,3},{8,12},{12,8},{9,1... | collective-permute-start | bytes 1572872 | tf_op jit(solution)/shard_map/ppermute | solution.py:956
  583.8 5.7 copy-start.30
  587.9 234.3 %collective-permute-start.22 = (bf16[3,4,256,512]{3,2,1,0:T(8,128)(2,1)S(1)}, bf16[3,4,256,512]{3,2,1,0:T(8,128)(2,1)}, u32[]{:S(2)}, u32[]{:S(2)}) collective-permute-start(bf16[3,4,256,512]{3,2,1,0:T(8,128)(2,1)S(1)} %add_convert_fusion.own_ref), channel_id=1, source_target_pairs={{0,4},{4,0},{1,5},{5,1},{2,6},{6,2},{3,7},{7,3},{8,12},{12,8},{9,1... | collective-permute-start | bytes 9437192 | tf_op jit(solution)/shard_map/ppermute | solution.py:956
  589.5 16.6 %copy-start.1 = (f32[512,1536]{1,0:T(8,128)S(1)}, f32[512,1536]{1,0:T(8,128)}, u32[]{:S(2)}) copy-start(f32[512,1536]{1,0:T(8,128)} %copy-done) | copy-start | bytes 9437188
  589.5 16.6 %copy-start.2 = (f32[1024,512]{1,0:T(8,128)S(1)}, f32[1024,512]{1,0:T(8,128)}, u32[]{:S(2)}) copy-start(f32[1024,512]{1,0:T(8,128)} %get-tuple-element.93.dk_ref) | copy-start | bytes 6291460
  589.5 16.6 %copy-start.3 = (f32[1024,512]{1,0:T(8,128)S(1)}, f32[1024,512]{1,0:T(8,128)}, u32[]{:S(2)}) copy-start(f32[1024,512]{1,0:T(8,128)} %get-tuple-element.94.dv_ref) | copy-start | bytes 6291460
  589.5 16.5 %copy-start.5 = (f32[512,128]{1,0:T(8,128)S(1)}, f32[512,128]{1,0:T(8,128)}, u32[]{:S(2)}) copy-start(f32[512,128]{1,0:T(8,128)} %copy-done.4) | copy-start | bytes 786436
  589.5 16.5 %copy-start.8 = (f32[512,512]{1,0:T(8,128)S(1)}, f32[512,512]{1,0:T(8,128)}, u32[]{:S(2)}) copy-start(f32[512,512]{1,0:T(8,128)} %copy-done.7) | copy-start | bytes 3145732
  589.5 16.5 %copy-start.12 = (f32[512,8]{1,0:T(8,128)S(1)}, f32[512,8]{1,0:T(8,128)}, u32[]{:S(2)}) copy-start(f32[512,8]{1,0:T(8,128)} %copy-done.11) | copy-start | bytes 49156
  594.3 222.1 %collective-permute-start.24 = (bf16[3,2,256,512]{3,2,1,0:T(8,128)(2,1)}, bf16[3,2,256,512]{3,2,1,0:T(8,128)(2,1)}, u32[]{:S(2)}, u32[]{:S(2)}) collective-permute-start(bf16[3,2,256,512]{3,2,1,0:T(8,128)(2,1)} %get-tuple-element.187.own_ref), channel_id=1, source_target_pairs={{0,4},{4,0},{1,5},{5,1},{2,6},{6,2},{3,7},{7,3},{8,12},{12,8},{9,1... | collective-permute-start | bytes 4718600 | tf_op jit(solution)/shard_map/ppermute | solution.py:956
  594.8 215.7 %collective-permute-start.25 = (bf16[3,2,256,512]{3,2,1,0:T(8,128)(2,1)}, bf16[3,2,256,512]{3,2,1,0:T(8,128)(2,1)}, u32[]{:S(2)}, u32[]{:S(2)}) collective-permute-start(bf16[3,2,256,512]{3,2,1,0:T(8,128)(2,1)} %get-tuple-element.186.own_ref), channel_id=1, source_target_pairs={{0,4},{4,0},{1,5},{5,1},{2,6},{6,2},{3,7},{7,3},{8,12},{12,8},{9,1... | collective-permute-start | bytes 4718600 | tf_op jit(solution)/shard_map/ppermute | solution.py:956
  632.9 124.1 %collective-permute-start.17 = (bf16[512,1664]{1,0:T(8,128)(2,1)}, bf16[512,1664]{1,0:T(8,128)(2,1)}, u32[]{:S(2)}, u32[]{:S(2)}) collective-permute-start(bf16[512,1664]{1,0:T(8,128)(2,1)} %get-tuple-element.109), channel_id=1, source_target_pairs={{0,16},{8,24},{16,0},{24,8},{1,17},{9,25},{17,1},{25,9},{2,18},{10... | collective-permute-start | bytes 5111816 | tf_op jit(solution)/shard_map/ppermute | solution.py:953
  640.8 116.1 %copy-start.43 = (f32[5120]{0:T(1024)S(1)}, f32[5120]{0:T(1024)}, u32[]{:S(2)}) copy-start(f32[5120]{0:T(1024)} %custom-call) | copy-start | bytes 61444
  760.1 71.2 %collective-permute-start.18 = (bf16[512,1664]{1,0:T(8,128)(2,1)}, bf16[512,1664]{1,0:T(8,128)(2,1)}, u32[]{:S(2)}, u32[]{:S(2)}) collective-permute-start(bf16[512,1664]{1,0:T(8,128)(2,1)} %add_convert_fusion.2), channel_id=1, source_target_pairs={{0,4},{4,0},{1,5},{5,1},{2,6},{6,2},{3,7},{7,3},{8,12},{12,8},{9,1... | collective-permute-start | bytes 5111816 | tf_op jit(solution)/shard_map/ppermute | solution.py:956
  (12 other events, 17.8 us)
